TPU v7x, 32 devices: a 4x2x2 block of a 4x4x8 slice. The times are simulated.
32 devices in a mesh: dp: 4 (over y, z), sp: 8 (over x, core).
Axes of the slice: x: 4, y: 2, z: 2, core: 2. Of those that a mesh axis runs over, the one named last changes fastest.
The devices are a block of a 4x4x8 slice.
Arguments:
- x_in: bfloat16 [32, 512, 1024], P('dp', 'sp'), parts along dimension 0
- grad_y: bfloat16 [32, 512, 1024], P('dp', 'sp'), parts along dimension 0
- positions: int32 [2048], P(('dp', 'sp')), parts along dimension 0
- w_q: bfloat16 [1024, 2048], replicated
- w_k: bfloat16 [1024, 1024], replicated
- w_v: bfloat16 [1024, 1024], replicated
- w_o: bfloat16 [2048, 1024], replicated
- w_gate: bfloat16 [1024, 3072], replicated
- w_up: bfloat16 [1024, 3072], replicated
- w_down: bfloat16 [3072, 1024], replicated
- norm_gain: float32 [1024], replicated
- q_norm: float32 [16, 128], replicated
- k_norm: float32 [8, 128], replicated
Outputs:
- output 1: bfloat16 [32, 512, 1024], P('dp', 'sp'), parts along dimension 0
- output 2: bfloat16 [32, 512, 1024], P('dp', 'sp'), parts along dimension 0
- output 3: bfloat16 [4096, 2048], P('dp'), parts along dimension 0
- output 4: bfloat16 [4096, 1024], P('dp'), parts along dimension 0
- output 5: bfloat16 [4096, 1024], P('dp'), parts along dimension 0
- output 6: bfloat16 [8192, 1024], P('dp'), parts along dimension 0
- output 7: bfloat16 [4096, 3072], P('dp'), parts along dimension 0
- output 8: bfloat16 [4096, 3072], P('dp'), parts along dimension 0
- output 9: bfloat16 [12288, 1024], P('dp'), parts along dimension 0
- output 10: float32 [4096], P('dp'), parts along dimension 0
- output 11: float32 [64, 128], P('dp'), parts along dimension 0
- output 12: float32 [32, 128], P('dp'), parts along dimension 0
There are 4 independent parts. A program takes and returns all parts, laid end to end along the dimension named above; an argument that names none is the same for every part.
All inputs are finite; a program needn't handle non-finite values.
Results may differ from a plain program's by a relative error of at most 0.02.
Values are sent between devices in bfloat16 or wider.
A program may use at most 768 MiB of HBM per device.

v0:
```python
import functools

import jax
import jax.numpy as jnp
from jax import lax
from jax.experimental import pallas as pl
from jax.experimental.pallas import tpu as pltpu
from jax.sharding import PartitionSpec as P


NORM_EPS = 1e-5
ROPE_THETA = 75.0e6
F32 = jnp.float32
BF16 = jnp.bfloat16
MESH = pl.DeviceIdType.MESH


def dot_nn(lhs, rhs):
    return lax.dot_general(lhs, rhs, (((1,), (0,)), ((), ())), preferred_element_type=F32)


def dot_nt(lhs, rhs):
    return lax.dot_general(lhs, rhs, (((1,), (1,)), ((), ())), preferred_element_type=F32)


def swiglu_both(gate, up, d_hidden):
    sig = jax.nn.sigmoid(gate)
    act = gate * sig
    d_hidden = d_hidden.astype(BF16).astype(F32)
    d_gate = d_hidden * up * (sig * (1.0 + gate * (1.0 - sig)))
    return (act * up).astype(BF16), d_gate.astype(BF16), (d_hidden * act).astype(BF16)


def other_devices(count):
    me = lax.axis_index('sp')
    return [lax.rem(me + shift, count) for shift in range(1, count)]


def meet(count):
    barrier = pltpu.get_barrier_semaphore()
    for device in other_devices(count):
        pl.semaphore_signal(barrier, inc=1, device_id={'sp': device}, device_id_type=MESH)
    pl.semaphore_wait(barrier, count - 1)


def own_mlp_kernel(n_ref, dy_ref, wg_ref, wu_ref, wd_ref, rope_ref, m_ref, dn_ref, gn_ref, gdy_ref, rest_ref, grope_ref,
                   m_acc, send_sem, recv_sem, rope_send, rope_recv, local_sem, *, count):
    step = pl.program_id(0)
    last = pl.num_programs(0) - 1
    me = lax.axis_index('sp')
    right, left, across, partner = lax.rem(me + 2, count), lax.rem(me + count - 2, count), lax.rem(me + 4, count), me + 1 - 2 * lax.rem(me, 2)
    other = lambda device: device + 1 - 2 * lax.rem(device, 2)
    first = gn_ref.shape[1]
    rows = n_ref.shape[0]

    def send(index, src, into, slot, target):
        return pltpu.make_async_remote_copy(src_ref=src, dst_ref=into.at[slot], send_sem=send_sem.at[index], recv_sem=recv_sem.at[index],
                                            device_id={'sp': target}, device_id_type=MESH)

    def forward(index, ref, slot, target):
        return send(index, ref.at[slot], ref, slot, target)

    n_own, dy_own = n_ref.at[pl.ds(0, first)], dy_ref.at[pl.ds(0, first)]
    own_sends = lambda: [send(0, dy_own, gdy_ref, me, right), send(2, n_own, gn_ref, me, left), send(1, n_own, gn_ref, me, right),
                         send(3, dy_own, gdy_ref, me, left), send(4, n_own, gn_ref, me, partner), send(5, dy_own, gdy_ref, me, partner)]
    early = lambda: [forward(6, gdy_ref, left, right), forward(7, gn_ref, right, left), forward(8, gdy_ref, left, partner), forward(9, gn_ref, right, partner)]
    late = lambda: [forward(10, gn_ref, left, partner), forward(11, gdy_ref, right, partner), forward(12, gdy_ref, across, partner), forward(13, gn_ref, across, partner)]
    tables = lambda: [pltpu.make_async_remote_copy(src_ref=rope_ref, dst_ref=grope_ref.at[me], send_sem=rope_send.at[i], recv_sem=rope_recv.at[i],
                                                   device_id={'sp': device}, device_id_type=MESH) for i, device in enumerate(other_devices(count))]
    keep = lambda: [pltpu.make_async_copy(n_own, gn_ref.at[me], local_sem.at[0]), pltpu.make_async_copy(dy_own, gdy_ref.at[me], local_sem.at[1]),
                    pltpu.make_async_copy(n_ref.at[pl.ds(first, rows - first)], rest_ref.at[0], local_sem.at[2]),
                    pltpu.make_async_copy(dy_ref.at[pl.ds(first, rows - first)], rest_ref.at[1], local_sem.at[3]),
                    pltpu.make_async_copy(rope_ref, grope_ref.at[me], local_sem.at[4])]

    def arrived(index, ref, slot):
        send(index, ref.at[slot], ref, slot, partner).wait_recv()

    @pl.when(step == 0)
    def _():
        meet(count)
        for copy in own_sends() + tables() + keep():
            copy.start()

    @pl.when(step == last - 1)
    def _():
        arrived(0, gdy_ref, left)
        arrived(2, gn_ref, right)
        for copy in early():
            copy.start()

    n, dy = n_ref[...], dy_ref[...]
    wg, wu, wd = wg_ref[...], wu_ref[...], wd_ref[...]
    hidden, d_gate, d_up = swiglu_both(dot_nn(n, wg), dot_nn(n, wu), dot_nt(dy, wd))
    m_new = dot_nn(hidden, wd)
    dn_new = dot_nt(d_gate, wg) + dot_nt(d_up, wu)

    @pl.when(step == 0)
    def _():
        m_acc[...] = m_new
        dn_ref[...] = dn_new

    @pl.when(step > 0)
    def _():
        m_acc[...] += m_new
        dn_ref[...] += dn_new

    @pl.when(step == last)
    def _():
        m_ref[...] = m_acc[...].astype(BF16)
        late_copies = late()
        for copy, (index, ref, slot) in zip(late_copies, ((1, gn_ref, left), (3, gdy_ref, right), (6, gdy_ref, across), (7, gn_ref, across))):
            arrived(index, ref, slot)
            copy.start()
        for index, ref, slot in ((4, gn_ref, partner), (5, gdy_ref, partner), (8, gdy_ref, other(left)), (9, gn_ref, other(right)),
                                 (10, gn_ref, other(left)), (11, gdy_ref, other(right)), (12, gdy_ref, other(across)), (13, gn_ref, other(across))):
            arrived(index, ref, slot)
        for copy in own_sends() + early() + late_copies:
            copy.wait_send()
        for copy in tables():
            copy.wait()
        for copy in keep():
            copy.wait()


def own_mlp(n, dy, w_gate, w_up, w_down, rope, count, first, block):
    rows, model = n.shape
    ffn = w_gate.shape[1]
    whole = pl.BlockSpec((rows, model), lambda i: (0, 0))
    cols = pl.BlockSpec((model, block), lambda i: (0, i))
    away = pl.BlockSpec(memory_space=pl.ANY)
    dma = pltpu.SemaphoreType.DMA
    return pl.pallas_call(
        functools.partial(own_mlp_kernel, count=count),
        grid=(ffn // block,),
        in_specs=[whole, whole, cols, cols, pl.BlockSpec((block, model), lambda i: (i, 0)), pl.BlockSpec(rope.shape, lambda i: (0, 0, 0))],
        out_specs=[whole, whole, away, away, away, away],
        out_shape=[jax.ShapeDtypeStruct((rows, model), BF16), jax.ShapeDtypeStruct((rows, model), F32),
                   jax.ShapeDtypeStruct((count, first, model), BF16), jax.ShapeDtypeStruct((count, first, model), BF16),
                   jax.ShapeDtypeStruct((2, rows - first, model), BF16), jax.ShapeDtypeStruct((count,) + rope.shape, F32)],
        scratch_shapes=[pltpu.VMEM((rows, model), F32), dma((14,)), dma((14,)), dma((count - 1,)), dma((count - 1,)), dma((5,))],
        compiler_params=pltpu.CompilerParams(vmem_limit_bytes=50 * 2 ** 20, collective_id=0, has_side_effects=True),
        cost_estimate=pl.CostEstimate(flops=12 * rows * model * ffn, bytes_accessed=6 * model * ffn, transcendentals=0),
    )(n, dy, w_gate, w_up, w_down, rope)


def all_mlp_kernel(*refs, chunks, block, count):
    n_refs, dy_refs = refs[:chunks], refs[chunks:2 * chunks]
    (wg_ref, wu_ref, wd_ref, mix_ref, gg_ref, gu_ref, gd_ref, pg_ref, pu_ref, pd_ref, swap_ref,
     n_all, dy_all, n_t, dy_t, acc_g, acc_u, acc_d, swap_send, swap_recv, half_send, half_recv, own_sem) = refs[2 * chunks:]
    step = pl.program_id(0)
    last = pl.num_programs(0) - 1
    share = wg_ref.shape[1]
    me = lax.axis_index('sp')
    partner = me + 1 - 2 * lax.rem(me, 2)

    def swaps():
        return [pltpu.make_async_remote_copy(src_ref=mix_ref.at[device], dst_ref=swap_ref.at[me], send_sem=swap_send.at[i], recv_sem=swap_recv.at[i],
                                             device_id={'sp': device}, device_id_type=MESH) for i, device in enumerate(other_devices(count))]

    def halves(i):
        cols = pl.ds(i * block, block)
        return [pltpu.make_async_remote_copy(src_ref=src.at[index], dst_ref=dst.at[index], send_sem=half_send.at[i, j], recv_sem=half_recv.at[i, j],
                                             device_id={'sp': partner}, device_id_type=MESH)
                for j, (src, dst, index) in enumerate(((gg_ref, pg_ref, (slice(None), cols)), (gu_ref, pu_ref, (slice(None), cols)), (gd_ref, pd_ref, (cols,))))]

    keep = lambda: pltpu.make_async_copy(mix_ref.at[me], swap_ref.at[me], own_sem)

    @pl.when(step == 0)
    def _():
        meet(count)
        keep().start()
        for copy in swaps():
            copy.start()
        acc_g[...] = jnp.zeros_like(acc_g)
        acc_u[...] = jnp.zeros_like(acc_u)
        acc_d[...] = jnp.zeros_like(acc_d)

    start = 0
    for n_ref, dy_ref in zip(n_refs, dy_refs):
        size = n_ref.shape[-2]
        n_all[start:start + size, :] = n_ref[...].reshape(size, n_ref.shape[-1])
        dy_all[start:start + size, :] = dy_ref[...].reshape(size, n_ref.shape[-1])
        start += size
    n_t[...] = n_all[...].T
    dy_t[...] = dy_all[...].T

    @pl.loop(0, share // block)
    def _(i):
        cols = pl.ds(pl.multiple_of(i * block, block), block)
        n, dy = n_all[...], dy_all[...]
        hidden, d_gate, d_up = swiglu_both(dot_nn(n, wg_ref[:, cols]), dot_nn(n, wu_ref[:, cols]), dot_nt(dy, wd_ref[cols, :]))
        acc_g[:, cols] += dot_nn(n_t[...], d_gate)
        acc_u[:, cols] += dot_nn(n_t[...], d_up)
        acc_d[:, cols] += dot_nn(dy_t[...], hidden)

        @pl.when(step == last)
        def _():
            gg_ref[:, cols] = acc_g[:, cols].astype(BF16)
            gu_ref[:, cols] = acc_u[:, cols].astype(BF16)
            gd_ref[cols, :] = acc_d[:, cols].T.astype(BF16)

        for done in range(share // block - 1):
            @pl.when((step == last) & (i == done + 1))
            def _():
                for copy in halves(done):
                    copy.start()

    @pl.when(step == last)
    def _():
        for copy in swaps():
            copy.wait()
        keep().wait()
        for copy in halves(share // block - 1):
            copy.start()
        for i in range(share // block):
            for copy in halves(i):
                copy.wait()


def all_mlp(n_chunks, dy_chunks, w_gate, w_up, w_down, mix, block):
    count, _, model = n_chunks[0][0].shape[-3:]
    share = w_gate.shape[1] // 2

    def rows_of(part, which):
        if part.ndim == 3:
            return pl.BlockSpec((1,) + part.shape[1:], lambda i: (i, 0, 0))
        return pl.BlockSpec((1, 1) + part.shape[2:], lambda i: (i, which, 0, 0))

    chunks = n_chunks + dy_chunks
    tile = sum(part.shape[-2] for part, _ in n_chunks)
    one = pl.Buffered(1)
    core = lambda: lax.rem(lax.axis_index('sp'), 2)
    in_cols = pl.BlockSpec((model, share), lambda i: (0, core()), pipeline_mode=one)
    out_cols = pl.BlockSpec((model, share), lambda i: (0, 0), pipeline_mode=one)
    away = pl.BlockSpec(memory_space=pl.ANY)
    dma = pltpu.SemaphoreType.DMA
    grads = [jax.ShapeDtypeStruct((model, share), BF16), jax.ShapeDtypeStruct((model, share), BF16), jax.ShapeDtypeStruct((share, model), BF16)]
    return pl.pallas_call(
        functools.partial(all_mlp_kernel, chunks=len(n_chunks), block=block, count=count),
        grid=(count,),
        in_specs=[rows_of(*chunk) for chunk in chunks] + [in_cols, in_cols, pl.BlockSpec((share, model), lambda i: (core(), 0), pipeline_mode=one), away],
        out_specs=[out_cols, out_cols, pl.BlockSpec((share, model), lambda i: (0, 0), pipeline_mode=one)] + [away] * 4,
        out_shape=grads + grads + [jax.ShapeDtypeStruct(mix.shape, BF16)],
        scratch_shapes=[pltpu.VMEM((tile, model), BF16)] * 2 + [pltpu.VMEM((model, tile), BF16)] * 2 + [pltpu.VMEM((model, share), F32)] * 3
        + [dma((count - 1,)), dma((count - 1,)), dma((share // block, 3)), dma((share // block, 3)), dma],
        compiler_params=pltpu.CompilerParams(vmem_limit_bytes=61 * 2 ** 20, collective_id=1, has_side_effects=True),
        cost_estimate=pl.CostEstimate(flops=12 * count * tile * model * share, bytes_accessed=4 * model * count * tile + 12 * model * share, transcendentals=0),
    )(*[part for part, _ in chunks], w_gate, w_up, w_down, mix)


def swap_pairs(rows):
    width = rows.shape[1]
    lane = lax.broadcasted_iota(jnp.int32, rows.shape, 1)
    return jnp.where(lane % 2 == 0, pltpu.roll(rows, width - 1, 1), pltpu.roll(rows, 1, 1))


def head_forward(rows, weight, cos_t, sin_t):
    rows = rows.astype(F32)
    centered = rows - jnp.mean(rows, axis=-1, keepdims=True)
    scale = lax.rsqrt(jnp.mean(centered * centered, axis=-1, keepdims=True) + NORM_EPS)
    unit = centered * scale
    normed = unit * weight
    return (normed * cos_t + swap_pairs(normed) * sin_t).astype(BF16), unit, scale


def head_backward(grad, unit, scale, weight, cos_t, sin_t):
    grad = grad.astype(BF16).astype(F32)
    grad = grad * cos_t - swap_pairs(grad) * sin_t
    weight_grad = jnp.sum(grad * unit, axis=0, keepdims=True)
    grad = grad * weight
    along = jnp.mean(grad * unit, axis=-1, keepdims=True)
    grad = scale * (grad - jnp.mean(grad, axis=-1, keepdims=True) - unit * along)
    return grad.astype(BF16), weight_grad


def heads_kernel(me_ref, n_ref, dy_ref, wq_ref, wk_ref, wv_ref, wo_ref, cos_ref, sin_ref, qn_ref, kn_ref, *refs, heads, dim, block, first, last):
    sums, refs = ((), refs) if first else (refs[:3], refs[3:])
    mix_ref, wn_ref, *grad_refs, k_acc, v_acc, qkv_acc, o_acc = refs
    step = pl.program_id(0)
    pieces, piece, model = n_ref.shape[0], *n_ref.shape[-2:]
    full = pieces * piece
    cos_t, sin_t = cos_ref[...].reshape(full, dim), sin_ref[...].reshape(full, dim)
    score_scale = dim ** -0.5
    width = heads * dim

    def put(start, rows):
        mix_ref[:, 0, :, start:start + rows.shape[1]] = rows.reshape(pieces, piece, rows.shape[1])

    @pl.when(step == 0)
    def _():
        for into, given in zip((wn_ref, qkv_acc, o_acc), sums or (None,) * 3):
            into[...] = jnp.zeros_like(into) if given is None else given[...]

    n_rows = n_ref[...].reshape(full, model)
    dy_rows = dy_ref[...].reshape(full, model)
    q_proj = dot_nn(n_rows, wq_ref[...]).astype(BF16)
    k_proj = dot_nn(n_rows, wk_ref[...]).astype(BF16)
    v_rows = dot_nn(n_rows, wv_ref[...]).astype(BF16)
    d_out = dot_nt(dy_rows, wo_ref[...]).astype(BF16)
    q_weights = [qn_ref[pl.ds(me_ref[0] * heads + h, 1), :] for h in range(heads)]
    k_weight = kn_ref[pl.ds(me_ref[0], 1), :]
    q_parts = [head_forward(q_proj[:, h * dim:(h + 1) * dim], q_weights[h], cos_t, sin_t) for h in range(heads)]
    k_rot, k_unit, k_scale = head_forward(k_proj, k_weight, cos_t, sin_t)
    k_t, v_t = k_rot.T, v_rows.T
    o_blocks, dq_blocks = [[] for _ in range(heads)], [[] for _ in range(heads)]
    for start in range(full - block, -1, -block):
        stop = start + block
        q_blk = jnp.concatenate([q_parts[h][0][start:stop] for h in range(heads)], axis=0)
        do_blk = jnp.concatenate([d_out[start:stop, h * dim:(h + 1) * dim] for h in range(heads)], axis=0)
        k_blk, v_blk = k_rot[:stop], v_rows[:stop]
        scores = dot_nt(k_blk, q_blk)
        tail = scores[start:]
        key = lax.broadcasted_iota(jnp.int32, tail.shape, 0)
        query = lax.broadcasted_iota(jnp.int32, tail.shape, 1) % block
        tail = jnp.where(query >= key, tail, -1e30)
        scores = tail if start == 0 else jnp.concatenate([scores[:start], tail], axis=0)
        top = jnp.max(scores, axis=0, keepdims=True)
        probs = jnp.exp((scores - top) * score_scale)
        probs = probs * (1.0 / jnp.sum(probs, axis=0, keepdims=True))
        probs_b = probs.astype(BF16)
        o_blk = dot_nn(v_t[:, :stop], probs_b).astype(BF16)
        d_probs = dot_nt(v_blk, do_blk)
        delta = jnp.sum(probs * d_probs, axis=0, keepdims=True)
        d_scores = (probs * (d_probs - delta)).astype(BF16)
        dq_blk = dot_nn(k_t[:, :stop], d_scores) * score_scale
        dk_new, dv_new = dot_nn(d_scores, q_blk), dot_nn(probs_b, do_blk)
        if stop == full:
            k_acc[...], v_acc[...] = dk_new, dv_new
        else:
            k_acc[0:stop, :] += dk_new
            v_acc[0:stop, :] += dv_new
        for h in range(heads):
            o_blocks[h].append(o_blk[:, h * block:(h + 1) * block])
            dq_blocks[h].append(dq_blk[:, h * block:(h + 1) * block].T)
    for h in range(heads):
        o_t = jnp.concatenate(o_blocks[h][::-1], axis=1)
        put(h * dim, o_t.T)
        o_acc[h * dim:(h + 1) * dim, :] += dot_nn(o_t, dy_rows)
        _, unit, scale = q_parts[h]
        dq, weight_grad = head_backward(jnp.concatenate(dq_blocks[h][::-1], axis=0), unit, scale, q_weights[h], cos_t, sin_t)
        put(width + h * dim, dq)
        qkv_acc[h * dim:(h + 1) * dim, :] += dot_nn(dq.T, n_rows)
        wn_ref[h:h + 1, :] += weight_grad
    dk, weight_grad = head_backward(k_acc[...] * score_scale, k_unit, k_scale, k_weight, cos_t, sin_t)
    wn_ref[heads:heads + 1, :] += weight_grad
    dv = v_acc[...].astype(BF16)
    put(2 * width, dk)
    put(2 * width + dim, dv)
    qkv_acc[width:width + dim, :] += dot_nn(dk.T, n_rows)
    qkv_acc[width + dim:width + 2 * dim, :] += dot_nn(dv.T, n_rows)

    @pl.when(step == pl.num_programs(0) - 1)
    def _():
        if last:
            packed, = grad_refs
            qkv_size = qkv_acc.shape[0]
            size = o_acc.shape[0]
            packed[:, :qkv_size] = qkv_acc[...].T.astype(BF16)
            for i in range(model // size):
                packed[i * size:(i + 1) * size, qkv_size:] = o_acc[:, i * size:(i + 1) * size].astype(BF16)
        else:
            grad_refs[0][...] = qkv_acc[...]
            grad_refs[1][...] = o_acc[...]


def own_heads(me, n, dy, which, w_q, w_k, w_v, w_o, rope, q_norm, k_norm, sums, last):
    pieces, batch, piece, model = n.shape[0], *n.shape[-3:]
    num_heads, dim = q_norm.shape
    heads = num_heads // k_norm.shape[0]
    full = pieces * piece
    width = (heads + 2) * dim

    def seq(part, side):
        if part.ndim == 4:
            return pl.BlockSpec((pieces, 1, piece, model), lambda b, p: (0, b, 0, 0))
        return pl.BlockSpec((pieces, 1, 1, piece, model), lambda b, p: (0, side, b, 0, 0))

    whole = lambda shape: pl.BlockSpec(shape, lambda b, p: (0,) * len(shape))
    cols = lambda size: pl.BlockSpec((model, size), lambda b, p: (0, p[0]))
    table = lambda side: pl.BlockSpec((pieces, 1, piece, dim), lambda b, p: (0, side, 0, 0))
    mix_width = heads * dim + width
    if last:
        grads = [jax.ShapeDtypeStruct((model, mix_width), BF16)]
    else:
        grads = [jax.ShapeDtypeStruct((width, model), F32), jax.ShapeDtypeStruct((heads * dim, model), F32)]
    return pl.pallas_call(
        functools.partial(heads_kernel, heads=heads, dim=dim, block=min(128, full), first=not sums, last=last),
        grid_spec=pltpu.PrefetchScalarGridSpec(
            num_scalar_prefetch=1,
            grid=(batch,),
            in_specs=[seq(n, which[0]), seq(dy, which[1]), cols(heads * dim), cols(dim), cols(dim), pl.BlockSpec((heads * dim, model), lambda b, p: (p[0], 0)),
                      table(0), table(1), whole(q_norm.shape), whole(k_norm.shape)] + [whole(part.shape) for part in sums],
            out_specs=[pl.BlockSpec((pieces, 1, piece, mix_width), lambda b, p: (0, b, 0, 0)), whole((8, dim))] + [whole(part.shape) for part in grads],
            scratch_shapes=[pltpu.VMEM((full, dim), F32), pltpu.VMEM((full, dim), F32), pltpu.VMEM((width, model), F32), pltpu.VMEM((heads * dim, model), F32)],
        ),
        out_shape=[jax.ShapeDtypeStruct((pieces, batch, piece, mix_width), BF16), jax.ShapeDtypeStruct((8, dim), F32)] + grads,
        compiler_params=pltpu.CompilerParams(vmem_limit_bytes=56 * 2 ** 20),
        cost_estimate=pl.CostEstimate(flops=batch * full * (14 * heads * full * dim + 4 * model * (width + heads * dim)),
                                      bytes_accessed=4 * batch * full * model, transcendentals=0),
    )(me, n, dy, w_q, w_k, w_v, w_o, rope, rope, q_norm, k_norm, *sums)


def norm_kernel(x_ref, gain_ref, n_ref):
    x = x_ref[...].astype(F32)
    centered = x - jnp.mean(x, axis=-1, keepdims=True)
    scale = lax.rsqrt(jnp.mean(centered * centered, axis=-1, keepdims=True) + NORM_EPS)
    n_ref[...] = (centered * scale * gain_ref[...]).astype(BF16)


def input_norm(x, gain):
    rows, model = x.shape
    tile = rows // 4
    return pl.pallas_call(
        norm_kernel,
        grid=(rows // tile,),
        in_specs=[pl.BlockSpec((tile, model), lambda i: (i, 0)), pl.BlockSpec((1, model), lambda i: (0, 0))],
        out_specs=pl.BlockSpec((tile, model), lambda i: (i, 0)),
        out_shape=jax.ShapeDtypeStruct((rows, model), BF16),
        cost_estimate=pl.CostEstimate(flops=8 * rows * model, bytes_accessed=4 * rows * model, transcendentals=0),
    )(x, gain)


def finish_kernel(core_ref, *refs, chunks, parts):
    mix_refs = refs[:chunks]
    (x_ref, dy_ref, m_ref, dn_ref, gain_ref, wq_ref, wk_ref, wv_ref, wo_ref, packed_ref, gg_ref, gu_ref, gd_ref, pg_ref, pu_ref, pd_ref,
     y_ref, dx_ref, gain_grad_ref, fq_ref, fk_ref, fv_ref, fo_ref, fg_ref, fu_ref, fd_ref,
     mix, a_acc, d_acc, packed_buf, col_buf, row_buf, in_sem, out_sem) = refs[chunks:]
    step = pl.program_id(0)
    steps = pl.num_programs(0)
    o_size, k_size = parts
    share = gg_ref.shape[1]
    col_rows, row_rows = col_buf.shape[2], row_buf.shape[2]
    core = core_ref[0]

    def fetches(at):
        slot = lax.rem(at, 2)
        cols = pl.ds(pl.multiple_of(at * col_rows, col_rows), col_rows)
        rows = pl.ds(pl.multiple_of(at * row_rows, row_rows), row_rows)
        pairs = [(packed_ref.at[at], packed_buf.at[slot])]
        pairs += [(ref.at[cols], col_buf.at[slot, i]) for i, ref in enumerate((gg_ref, gu_ref, pg_ref, pu_ref))]
        pairs += [(ref.at[rows], row_buf.at[slot, i]) for i, ref in enumerate((gd_ref, pd_ref))]
        return [pltpu.make_async_copy(src, dst, in_sem.at[slot, i]) for i, (src, dst) in enumerate(pairs)]

    def places(at):
        slot = lax.rem(at, 2)
        buf = packed_buf.at[slot]
        model = buf.shape[0]
        at_o, at_k = pl.ds(pl.multiple_of(at * o_size, o_size), o_size), pl.ds(pl.multiple_of(at * k_size, k_size), k_size)
        pairs = [(buf.at[:, pl.ds(0, o_size)], fq_ref.at[:, at_o]), (buf.at[:, pl.ds(o_size, k_size)], fk_ref.at[:, at_k]),
                 (buf.at[:, pl.ds(o_size + k_size, k_size)], fv_ref.at[:, at_k])]
        pairs += [(buf.at[pl.ds(i * o_size, o_size), pl.ds(o_size + 2 * k_size, o_size)], fo_ref.at[at_o, pl.ds(i * o_size, o_size)]) for i in range(model // o_size)]
        cols = pl.ds(pl.multiple_of(at * col_rows, col_rows), col_rows)
        mine, theirs = pl.multiple_of(core * share, share), pl.multiple_of((1 - core) * share, share)
        pairs += [(col_buf.at[slot, i], ref.at[cols, pl.ds(start, share)]) for i, (ref, start) in enumerate(((fg_ref, mine), (fu_ref, mine), (fg_ref, theirs), (fu_ref, theirs)))]
        pairs += [(row_buf.at[slot, i], fd_ref.at[pl.ds(pl.multiple_of(start + at * row_rows, row_rows), row_rows)]) for i, start in enumerate((mine, theirs))]
        return [pltpu.make_async_copy(src, dst, out_sem.at[slot, i]) for i, (src, dst) in enumerate(pairs)]

    @pl.when(step == 0)
    def _():
        for copy in fetches(0):
            copy.start()

    start = 0
    for ref in mix_refs:
        mix[start:start + ref.shape[1], :] = ref[0]
        start += ref.shape[1]
    a_new = dot_nn(mix[:, :o_size], wo_ref[...])
    d_new = dot_nt(mix[:, o_size:2 * o_size], wq_ref[...])
    d_new += dot_nt(mix[:, 2 * o_size:2 * o_size + k_size], wk_ref[...]) + dot_nt(mix[:, 2 * o_size + k_size:], wv_ref[...])

    @pl.when(step == 0)
    def _():
        a_acc[...] = a_new
        d_acc[...] = d_new + dn_ref[...]

    @pl.when(step > 0)
    def _():
        a_acc[...] += a_new
        d_acc[...] += d_new

    for copy in fetches(step):
        copy.wait()
    for copy in places(step):
        copy.start()

    @pl.when(step > 0)
    def _():
        for copy in places(step - 1):
            copy.wait()

    @pl.when(step < steps - 1)
    def _():
        for copy in fetches(step + 1):
            copy.start()

    @pl.when(step == steps - 1)
    def _():
        x = x_ref[...].astype(F32)
        y_ref[...] = (x + a_acc[...].astype(BF16).astype(F32) + m_ref[...].astype(F32)).astype(BF16)
        centered = x - jnp.mean(x, axis=-1, keepdims=True)
        scale = lax.rsqrt(jnp.mean(centered * centered, axis=-1, keepdims=True) + NORM_EPS)
        unit = centered * scale
        grad = d_acc[...].astype(BF16).astype(F32)
        gain_grad_ref[...] = jnp.sum(grad * unit, axis=0, keepdims=True)
        grad = grad * gain_ref[...]
        along = jnp.mean(grad * unit, axis=-1, keepdims=True)
        grad = scale * (grad - jnp.mean(grad, axis=-1, keepdims=True) - unit * along)
        dx_ref[...] = (dy_ref[...].astype(F32) + grad).astype(BF16)
        for copy in places(step):
            copy.wait()


def finish(core, mixes, x, dy, mlp_out, d_norm, gain, w_q, w_k, w_v, w_o, packed, own_grads, partner_grads, o_size, k_size):
    rows, model = x.shape
    pieces, _, width = mixes[0].shape
    share = own_grads[0].shape[1]
    whole = pl.BlockSpec((rows, model), lambda i, c: (0, 0))
    row = pl.BlockSpec((1, model), lambda i, c: (0, 0))
    cols = lambda size: pl.BlockSpec((model, size), lambda i, c: (0, i))
    away = pl.BlockSpec(memory_space=pl.ANY)
    bf16 = lambda *shape: jax.ShapeDtypeStruct(shape, BF16)
    return pl.pallas_call(
        functools.partial(finish_kernel, chunks=len(mixes), parts=(o_size, k_size)),
        grid_spec=pltpu.PrefetchScalarGridSpec(
            num_scalar_prefetch=1,
            grid=(pieces,),
            in_specs=[pl.BlockSpec((1, mix.shape[1], width), lambda i, c: (i, 0, 0)) for mix in mixes] + [whole] * 4
            + [row, cols(o_size), cols(k_size), cols(k_size), pl.BlockSpec((o_size, model), lambda i, c: (i, 0))] + [away] * 7,
            out_specs=[whole, whole, row] + [away] * 7,
            scratch_shapes=[pltpu.VMEM((rows, width), BF16), pltpu.VMEM((rows, model), F32), pltpu.VMEM((rows, model), F32),
                            pltpu.VMEM((2,) + packed.shape[1:], BF16), pltpu.VMEM((2, 4, model // pieces, share), BF16), pltpu.VMEM((2, 2, share // pieces, model), BF16),
                            pltpu.SemaphoreType.DMA((2, 7)), pltpu.SemaphoreType.DMA((2, 9 + model // o_size))],
        ),
        out_shape=[bf16(rows, model), bf16(rows, model), jax.ShapeDtypeStruct((1, model), F32)]
        + [bf16(*weight.shape) for weight in (w_q, w_k, w_v, w_o)] + [bf16(model, 2 * share), bf16(model, 2 * share), bf16(2 * share, model)],
        compiler_params=pltpu.CompilerParams(vmem_limit_bytes=56 * 2 ** 20),
        cost_estimate=pl.CostEstimate(flops=2 * pieces * rows * width * model, bytes_accessed=14 * rows * model + 2 * pieces * width * (rows + model), transcendentals=0),
    )(core, *mixes, x, dy, mlp_out, d_norm, gain, w_q, w_k, w_v, w_o, packed, *own_grads, *partner_grads)


def share_kernel(part_ref, all_ref, send_sem, recv_sem, *, count):
    me = lax.axis_index('sp')
    meet(count)
    all_ref[pl.ds(me, 1)] = part_ref[...][None]
    copies = [pltpu.make_async_remote_copy(src_ref=part_ref, dst_ref=all_ref.at[me], send_sem=send_sem.at[i], recv_sem=recv_sem.at[i],
                                           device_id={'sp': device}, device_id_type=MESH) for i, device in enumerate(other_devices(count))]
    for copy in copies:
        copy.start()
    for copy in copies:
        copy.wait()


def share_small(part, count):
    vmem = pl.BlockSpec(memory_space=pltpu.VMEM)
    return pl.pallas_call(
        functools.partial(share_kernel, count=count),
        in_specs=[vmem],
        out_specs=vmem,
        out_shape=jax.ShapeDtypeStruct((count,) + part.shape, part.dtype),
        scratch_shapes=[pltpu.SemaphoreType.DMA((count - 1,)), pltpu.SemaphoreType.DMA((count - 1,))],
        compiler_params=pltpu.CompilerParams(collective_id=2, has_side_effects=True),
    )(part)


def solution(mesh):
    n_sp = mesh.shape['sp']
    seq_spec = P('dp', 'sp', None)
    grad_spec = P('dp', None)

    def layer_step(x_in, grad_y, positions, w_q, w_k, w_v, w_o, w_gate, w_up, w_down, norm_gain, q_norm, k_norm):
        batch, piece, model = x_in.shape
        num_heads, dim = q_norm.shape
        heads = num_heads // k_norm.shape[0]
        ffn = w_gate.shape[1]
        tokens = batch * piece
        me = lax.axis_index('sp')
        me_arr = me.reshape(1)
        split = (batch * 5) // 8
        gain_row = norm_gain.reshape(1, model)
        x_rows, dy_own = x_in.reshape(tokens, model), grad_y.reshape(tokens, model)
        n_own = input_norm(x_rows, gain_row)

        inv_freq = ROPE_THETA ** (-(jnp.arange(dim // 2, dtype=F32) * 2.0) / dim)
        angles = jnp.repeat(positions.astype(F32)[:, None] * inv_freq[None, :], 2, axis=1)
        sign = jnp.where(jnp.arange(dim) % 2 == 0, -1.0, 1.0).astype(F32)
        rope_own = jnp.stack([jnp.cos(angles), jnp.sin(angles) * sign[None, :]])

        mlp_out, d_norm, n_0, dy_0, rest, rope = own_mlp(n_own, dy_own, w_gate, w_up, w_down, rope_own, n_sp, split * piece, min(512, ffn))
        rest = lax.all_gather(rest, 'sp', axis=0, tiled=False)

        by_seq = lambda part: part.reshape(part.shape[:-2] + (-1, piece, part.shape[-1]))
        mix_0, *sums = own_heads(me_arr, by_seq(n_0), by_seq(dy_0), (0, 0), w_q, w_k, w_v, w_o, rope, q_norm, k_norm, (), False)
        mix_0 = lax.all_to_all(mix_0, 'sp', 0, 0, tiled=True)
        mix_1, norm_grads, packed = own_heads(me_arr, by_seq(rest), by_seq(rest), (0, 1), w_q, w_k, w_v, w_o, rope, q_norm, k_norm, tuple(sums), True)
        packed_all = lax.all_gather(packed, 'sp', axis=0, tiled=False)

        rows = lambda part: part.reshape(n_sp, -1, part.shape[-1])
        *grads, mix_1 = all_mlp([(n_0, 0), (rest, 0)], [(dy_0, 0), (rest, 1)], w_gate, w_up, w_down, rows(mix_1), ffn // 6)

        y_out, grad_x, grad_gain, *full = finish((me % 2).reshape(1), (rows(mix_0), mix_1), x_rows, dy_own, mlp_out, d_norm, gain_row, w_q, w_k, w_v, w_o,
                                                 packed_all, grads[:3], grads[3:], heads * dim, dim)

        gain_rows = model // dim
        small = jnp.concatenate([grad_gain.reshape(gain_rows, dim), norm_grads], axis=0)
        small = share_small(small, n_sp)
        full_gain = jnp.sum(small[:, :gain_rows], axis=0).reshape(model)
        full_qn = small[:, gain_rows:gain_rows + heads].reshape(num_heads, dim)
        full_kn = small[:, gain_rows + heads]
        return (y_out.reshape(x_in.shape), grad_x.reshape(x_in.shape), *full, full_gain, full_qn, full_kn)

    in_specs = (seq_spec, seq_spec, P(('dp', 'sp'))) + (P(),) * 10
    out_specs = (seq_spec, seq_spec) + (grad_spec,) * 7 + (P('dp'), grad_spec, grad_spec)
    return jax.shard_map(layer_step, mesh=mesh, in_specs=in_specs, out_specs=out_specs, check_vma=False)
```

profile of v0, /device:TPU:81, one launch (start us, length us, event | category | flops | bytes accessed | tf_op | source)
XLA Modules:
  0.0 332.0 jit_solution(1152241738618302304)
XLA Ops:
  7.2 0.1 all-gather.5.cloned.1.call-start
  7.3 0.7 convert_element_type.3
  7.9 0.2 multiply_cosine_fusion
  8.2 0.1 copy.28
  8.3 0.1 copy.27
  8.4 3.8 %shard_map.220.n_ref = bf16[512,1024]{1,0:T(8,128)(2,1)} custom-call(bf16[512,1024]{1,0:T(8,128)(2,1)} %bitcast.25, f32[1,1024]{1,0:T(1,128)} %bitcast.31), custom_call_target="tpu_custom_call" | custom-call | flops 4194304 | bytes 2097152 | tf_op jit(solution)/shard_map/pallas_call | solution.py:413
  12.2 0.0 copy-start.2
  12.2 1.2 copy-done.2
  13.5 62.0 %shard_map.221 = (bf16[512,1024]{1,0:T(8,128)(2,1)S(1)}, f32[512,1024]{1,0:T(8,128)}, bf16[8,320,1024]{2,1,0:T(8,128)(2,1)}, bf16[8,320,1024]{2,1,0:T(8,128)(2,1...) custom-call(bf16[512,1024]{1,0:T(8,128)(2,1)S(1)} %copy-done.2, bf16[512,1024]{1,0:T(8,128)(2,1)} %bitcast.27, ...), custom_call_target="tpu_custom_call" | custom-call | flops 19327352832 | bytes 18874368 | tf_op jit(solution)/shard_map/pallas_call | solution.py:132
  75.5 0.0 copy-start
  75.5 0.8 copy-done
  76.3 0.0 copy-start.1
  76.3 1.0 copy-done.1
  77.3 0.1 all-gather.5.cloned.1.call-update
  77.4 0.1 all-gather.7.cloned.1.call-start
  77.4 37.4 %shard_map.222 = (bf16[8,5,64,768]{3,2,1,0:T(8,128)(2,1)}, f32[8,128]{1,0:T(8,128)}, f32[512,1024]{1,0:T(8,128)}, f32[256,1024]{1,0:T(8,128)}) custom-call(s32[1]{0:T(128)} %bitcast.1.me_ref, bf16[8,5,64,1024]{3,2,1,0:T(8,128)(2,1)} %bitcast.40, bf16[8,5,64,1024]{3,2,1,0:T(8,128)(2,1)} %bitcast.41, bf16[1024,2048]{1,0:T(8,128)(2,1)} %refs_7_.1, ...), custom_call_target="tpu_custom_call" | custom-call | flops 12750684160 | bytes 10485760 | tf_op jit(solution)/shard_map/pallas_call | solution.py:386
  114.8 2.2 all-gather.5.cloned.1.call-done
  117.0 24.8 %shard_map.223 = (bf16[8,3,64,768]{3,2,1,0:T(8,128)(2,1)}, f32[8,128]{1,0:T(8,128)}, bf16[1024,768]{1,0:T(8,128)(2,1)}) custom-call(s32[1]{0:T(128)} %bitcast.1.me_ref, bf16[8,2,3,64,1024]{4,3,2,1,0:T(8,128)(2,1)} %bitcast.20, bf16[8,2,3,64,1024]{4,3,2,1,0:T(8,128)(2,1)} %bitcast.21, bf16[1024,2048]{1,0:T(8,128)(2,1)} %refs_7_.1, ...), custom_call_target="tpu_custom_call" | custom-call | flops 7650410496 | bytes 6291456 | tf_op jit(solution)/shard_map/pallas_call | solution.py:386
  141.8 0.1 all-gather.7.cloned.1.call-update
  141.9 4.8 %all-to-all-start = ((bf16[8,5,64,768]{3,2,1,0:T(8,128)(2,1)}), bf16[8,5,64,768]{3,2,1,0:T(8,128)(2,1)}, u32[]{:S(2)}, u32[]{:S(2)}) async-start(bf16[8,5,64,768]{3,2,1,0:T(8,128)(2,1)} %get-tuple-element.45), calls=%async_computation | async-start | bytes 7864320 | tf_op jit(solution)/shard_map/all_to_all | solution.py:593
  146.8 131.3 %shard_map.224 = (bf16[1024,1536]{1,0:T(8,128)(2,1)}, bf16[1024,1536]{1,0:T(8,128)(2,1)}, bf16[1536,1024]{1,0:T(8,128)(2,1)}, bf16[1024,1536]{1,0:T(8,128)(2,1)}...) custom-call(bf16[8,320,1024]{2,1,0:T(8,128)(2,1)} %get-tuple-element.42.refs_0_, ...), custom_call_target="tpu_custom_call" | custom-call | flops 77309411328 | bytes 35651584 | tf_op jit(solution)/shard_map/pallas_call | solution.py:238
  278.1 0.0 all-to-all-done
  278.1 0.0 all-gather.7.cloned.1.call-done
  278.1 0.0 copy-start.3
  278.1 34.9 %shard_map.225 = (bf16[512,1024]{1,0:T(8,128)(2,1)}, bf16[512,1024]{1,0:T(8,128)(2,1)}, f32[1,1024]{1,0:T(1,128)}, bf16[1024,2048]{1,0:T(8,128)(2,1)}, bf16[1024...) custom-call(s32[1]{0:T(128)} %bitcast.core_ref, ...), custom_call_target="tpu_custom_call" | custom-call | flops 6442450944 | bytes 26214400 | tf_op jit(solution)/shard_map/pallas_call | solution.py:522
  313.0 0.0 copy-done.3
  313.0 1.3 pad_maximum_fusion.1.part_ref
  314.3 6.8 %shard_map.226 = f32[8,16,128]{2,1,0:T(8,128)} custom-call(f32[16,128]{1,0:T(8,128)} %pad_maximum_fusion.1.part_ref), custom_call_target="tpu_custom_call" | custom-call | tf_op jit(solution)/shard_map/pallas_call | solution.py:555
  321.0 1.4 slice.11
  322.4 1.4 slice_reduce_fusion
  323.8 1.4 slice.10
  (6 shorter events, 0.1 us)
Async XLA Ops:
  7.2 109.9 %all-gather.5.cloned.1.call-start = ((), (), s32[]{:S(2)}) async-start(), calls=%async_computation.1 | async-start | bytes 7077888 | tf_op jit(solution)/shard_map/all_gather | solution.py:589
  12.2 1.2 copy-start.2
  75.5 0.8 copy-start
  76.3 1.0 copy-start.1
  77.4 200.7 %all-gather.7.cloned.1.call-start = ((), (), s32[]{:S(2)}) async-start(), calls=%async_computation.2 | async-start | bytes 14155776 | tf_op jit(solution)/shard_map/all_gather | solution.py:595
  141.9 136.2 %all-to-all-start = ((bf16[8,5,64,768]{3,2,1,0:T(8,128)(2,1)}), bf16[8,5,64,768]{3,2,1,0:T(8,128)(2,1)}, u32[]{:S(2)}, u32[]{:S(2)}) async-start(bf16[8,5,64,768]{3,2,1,0:T(8,128)(2,1)} %get-tuple-element.45), calls=%async_computation | async-start | bytes 7864320 | tf_op jit(solution)/shard_map/all_to_all | solution.py:593
  278.1 34.9 %copy-start.3 = (f32[8,128]{1,0:T(8,128)S(1)}, f32[8,128]{1,0:T(8,128)}, u32[]{:S(2)}) copy-start(f32[8,128]{1,0:T(8,128)} %get-tuple-element.71) | copy-start | bytes 12292
Sparse Core Ops, SparseCore 0:
  77.5 39.5 all-gather.4
  142.0 123.3 all-gather.6
where the time goes:
time: 333 us; the launch traced here: 332 us
  Pallas kernels  301 us (90%)
  between operations  14.2 us (4%)
  local copies, waits for them, and re-layouts  5.9 us (2%)
  starting transfers between devices  4.96 us (1%)
  other arithmetic  3.54 us (1%)
    pallas_call x1, Pallas kernels, all_mlp(): pl.pallas_call(functools.partial(all_mlp_kernel, chunks=len(n_chunks), bl...  131 us
    pallas_call x2, Pallas kernels, own_heads(): pl.pallas_call(functools.partial(heads_kernel, heads=heads, dim=dim, bloc...  62.2 us
    pallas_call x1, Pallas kernels, own_mlp(): pl.pallas_call(functools.partial(own_mlp_kernel, count=count), grid=(ffn...  62 us
    pallas_call x1, Pallas kernels, finish(): pl.pallas_call(functools.partial(finish_kernel, chunks=len(mixes), parts=...  34.9 us
    pallas_call x1, Pallas kernels, share_small(): pl.pallas_call(functools.partial(share_kernel, count=count), in_specs=[vm...  6.75 us
  transfers between devices with their start and end apart: 3, of which 1 were waited for; matrix products, arithmetic and copies ran while one was open for 0% of the time, Pallas kernels for 51%

commit v1 on v0

v1 whole, which is shorter than its diff:
```python
import functools

import jax
import jax.numpy as jnp
from jax import lax
from jax.experimental import pallas as pl
from jax.experimental.pallas import tpu as pltpu
from jax.sharding import PartitionSpec as P

NORM_EPS = 1e-5
ROPE_THETA = 75.0e6
F32 = jnp.float32
BF16 = jnp.bfloat16
MESH = pl.DeviceIdType.MESH


def dot_nn(lhs, rhs):
    return lax.dot_general(lhs, rhs, (((1,), (0,)), ((), ())), preferred_element_type=F32)


def dot_nt(lhs, rhs):
    return lax.dot_general(lhs, rhs, (((1,), (1,)), ((), ())), preferred_element_type=F32)


def swiglu_both(gate, up, d_hidden):
    sig = jax.nn.sigmoid(gate)
    act = gate * sig
    d_hidden = d_hidden.astype(BF16).astype(F32)
    d_gate = d_hidden * up * (sig * (1.0 + gate * (1.0 - sig)))
    return (act * up).astype(BF16), d_gate.astype(BF16), (d_hidden * act).astype(BF16)


def other_devices(count):
    me = lax.axis_index('sp')
    return [lax.rem(me + shift, count) for shift in range(1, count)]


def meet(count):
    barrier = pltpu.get_barrier_semaphore()
    for device in other_devices(count):
        pl.semaphore_signal(barrier, inc=1, device_id={'sp': device}, device_id_type=MESH)
    pl.semaphore_wait(barrier, count - 1)


def all_mlp_kernel(*refs, chunks, block, count):
    n_refs, dy_refs = refs[:chunks], refs[chunks:2 * chunks]
    (wg_ref, wu_ref, wd_ref, mix_ref, gg_ref, gu_ref, gd_ref, pg_ref, pu_ref, pd_ref, swap_ref,
     n_all, dy_all, n_t, dy_t, acc_g, acc_u, acc_d, swap_send, swap_recv, half_send, half_recv, own_sem) = refs[2 * chunks:]
    step = pl.program_id(0)
    last = pl.num_programs(0) - 1
    share = wg_ref.shape[1]
    me = lax.axis_index('sp')
    partner = me + 1 - 2 * lax.rem(me, 2)

    def swaps():
        return [pltpu.make_async_remote_copy(src_ref=mix_ref.at[device], dst_ref=swap_ref.at[me], send_sem=swap_send.at[i], recv_sem=swap_recv.at[i],
                                             device_id={'sp': device}, device_id_type=MESH) for i, device in enumerate(other_devices(count))]

    def halves(i):
        cols = pl.ds(i * block, block)
        return [pltpu.make_async_remote_copy(src_ref=src.at[index], dst_ref=dst.at[index], send_sem=half_send.at[i, j], recv_sem=half_recv.at[i, j],
                                             device_id={'sp': partner}, device_id_type=MESH)
                for j, (src, dst, index) in enumerate(((gg_ref, pg_ref, (slice(None), cols)), (gu_ref, pu_ref, (slice(None), cols)), (gd_ref, pd_ref, (cols,))))]

    keep = lambda: pltpu.make_async_copy(mix_ref.at[me], swap_ref.at[me], own_sem)

    @pl.when(step == 0)
    def _():
        meet(count)
        keep().start()
        for copy in swaps():
            copy.start()
        acc_g[...] = jnp.zeros_like(acc_g)
        acc_u[...] = jnp.zeros_like(acc_u)
        acc_d[...] = jnp.zeros_like(acc_d)

    start = 0
    for n_ref, dy_ref in zip(n_refs, dy_refs):
        size = n_ref.shape[-2]
        n_all[start:start + size, :] = n_ref[...].reshape(size, n_ref.shape[-1])
        dy_all[start:start + size, :] = dy_ref[...].reshape(size, n_ref.shape[-1])
        start += size
    n_t[...] = n_all[...].T
    dy_t[...] = dy_all[...].T

    @pl.loop(0, share // block)
    def _(i):
        cols = pl.ds(pl.multiple_of(i * block, block), block)
        n, dy = n_all[...], dy_all[...]
        hidden, d_gate, d_up = swiglu_both(dot_nn(n, wg_ref[:, cols]), dot_nn(n, wu_ref[:, cols]), dot_nt(dy, wd_ref[cols, :]))
        acc_g[:, cols] += dot_nn(n_t[...], d_gate)
        acc_u[:, cols] += dot_nn(n_t[...], d_up)
        acc_d[:, cols] += dot_nn(dy_t[...], hidden)

        @pl.when(step == last)
        def _():
            gg_ref[:, cols] = acc_g[:, cols].astype(BF16)
            gu_ref[:, cols] = acc_u[:, cols].astype(BF16)
            gd_ref[cols, :] = acc_d[:, cols].T.astype(BF16)

        for done in range(share // block - 1):
            @pl.when((step == last) & (i == done + 1))
            def _():
                for copy in halves(done):
                    copy.start()

    @pl.when(step == last)
    def _():
        for copy in swaps():
            copy.wait()
        keep().wait()
        for copy in halves(share // block - 1):
            copy.start()
        for i in range(share // block):
            for copy in halves(i):
                copy.wait()


def all_mlp(n_chunks, dy_chunks, w_gate, w_up, w_down, mix, block):
    count, _, model = n_chunks[0][0].shape[-3:]
    share = w_gate.shape[1] // 2

    def rows_of(part, which):
        if part.ndim == 3:
            return pl.BlockSpec((1,) + part.shape[1:], lambda i: (i, 0, 0))
        return pl.BlockSpec((1, 1) + part.shape[2:], lambda i: (i, which, 0, 0))

    chunks = n_chunks + dy_chunks
    tile = sum(part.shape[-2] for part, _ in n_chunks)
    one = pl.Buffered(1)
    core = lambda: lax.rem(lax.axis_index('sp'), 2)
    in_cols = pl.BlockSpec((model, share), lambda i: (0, core()), pipeline_mode=one)
    out_cols = pl.BlockSpec((model, share), lambda i: (0, 0), pipeline_mode=one)
    away = pl.BlockSpec(memory_space=pl.ANY)
    dma = pltpu.SemaphoreType.DMA
    grads = [jax.ShapeDtypeStruct((model, share), BF16), jax.ShapeDtypeStruct((model, share), BF16), jax.ShapeDtypeStruct((share, model), BF16)]
    return pl.pallas_call(
        functools.partial(all_mlp_kernel, chunks=len(n_chunks), block=block, count=count),
        grid=(count,),
        in_specs=[rows_of(*chunk) for chunk in chunks] + [in_cols, in_cols, pl.BlockSpec((share, model), lambda i: (core(), 0), pipeline_mode=one), away],
        out_specs=[out_cols, out_cols, pl.BlockSpec((share, model), lambda i: (0, 0), pipeline_mode=one)] + [away] * 4,
        out_shape=grads + grads + [jax.ShapeDtypeStruct(mix.shape, BF16)],
        scratch_shapes=[pltpu.VMEM((tile, model), BF16)] * 2 + [pltpu.VMEM((model, tile), BF16)] * 2 + [pltpu.VMEM((model, share), F32)] * 3
        + [dma((count - 1,)), dma((count - 1,)), dma((share // block, 3)), dma((share // block, 3)), dma],
        compiler_params=pltpu.CompilerParams(vmem_limit_bytes=61 * 2 ** 20, collective_id=1, has_side_effects=True),
        cost_estimate=pl.CostEstimate(flops=12 * count * tile * model * share, bytes_accessed=4 * model * count * tile + 12 * model * share, transcendentals=0),
    )(*[part for part, _ in chunks], w_gate, w_up, w_down, mix)


def swap_pairs(rows):
    width = rows.shape[1]
    lane = lax.broadcasted_iota(jnp.int32, rows.shape, 1)
    return jnp.where(lane % 2 == 0, pltpu.roll(rows, width - 1, 1), pltpu.roll(rows, 1, 1))


def head_forward(rows, weight, cos_t, sin_t):
    rows = rows.astype(F32)
    centered = rows - jnp.mean(rows, axis=-1, keepdims=True)
    scale = lax.rsqrt(jnp.mean(centered * centered, axis=-1, keepdims=True) + NORM_EPS)
    unit = centered * scale
    normed = unit * weight
    return (normed * cos_t + swap_pairs(normed) * sin_t).astype(BF16), unit, scale


def head_backward(grad, unit, scale, weight, cos_t, sin_t):
    grad = grad.astype(BF16).astype(F32)
    grad = grad * cos_t - swap_pairs(grad) * sin_t
    weight_grad = jnp.sum(grad * unit, axis=0, keepdims=True)
    grad = grad * weight
    along = jnp.mean(grad * unit, axis=-1, keepdims=True)
    grad = scale * (grad - jnp.mean(grad, axis=-1, keepdims=True) - unit * along)
    return grad.astype(BF16), weight_grad


def one_sequence(me, n_rows, dy_rows, cos_t, sin_t, wq_ref, wk_ref, wv_ref, wo_ref, qn_ref, kn_ref, mix_ref, wn_ref, k_acc, v_acc, qkv_acc, o_acc, heads, dim, block):
    pieces, _, piece, _ = mix_ref.shape
    full = pieces * piece
    score_scale = dim ** -0.5
    width = heads * dim

    def put(start, rows):
        mix_ref[:, 0, :, start:start + rows.shape[1]] = rows.reshape(pieces, piece, rows.shape[1])

    q_proj = dot_nn(n_rows, wq_ref[...]).astype(BF16)
    k_proj = dot_nn(n_rows, wk_ref[...]).astype(BF16)
    v_rows = dot_nn(n_rows, wv_ref[...]).astype(BF16)
    d_out = dot_nt(dy_rows, wo_ref[...]).astype(BF16)
    q_weights = [qn_ref[pl.ds(me * heads + h, 1), :] for h in range(heads)]
    k_weight = kn_ref[pl.ds(me, 1), :]
    q_parts = [head_forward(q_proj[:, h * dim:(h + 1) * dim], q_weights[h], cos_t, sin_t) for h in range(heads)]
    k_rot, k_unit, k_scale = head_forward(k_proj, k_weight, cos_t, sin_t)
    k_t, v_t = k_rot.T, v_rows.T
    o_blocks, dq_blocks = [[] for _ in range(heads)], [[] for _ in range(heads)]
    for start in range(full - block, -1, -block):
        stop = start + block
        q_blk = jnp.concatenate([q_parts[h][0][start:stop] for h in range(heads)], axis=0)
        do_blk = jnp.concatenate([d_out[start:stop, h * dim:(h + 1) * dim] for h in range(heads)], axis=0)
        k_blk, v_blk = k_rot[:stop], v_rows[:stop]
        scores = dot_nt(k_blk, q_blk)
        tail = scores[start:]
        key = lax.broadcasted_iota(jnp.int32, tail.shape, 0)
        query = lax.broadcasted_iota(jnp.int32, tail.shape, 1) % block
        tail = jnp.where(query >= key, tail, -1e30)
        scores = tail if start == 0 else jnp.concatenate([scores[:start], tail], axis=0)
        top = jnp.max(scores, axis=0, keepdims=True)
        probs = jnp.exp((scores - top) * score_scale)
        probs = probs * (1.0 / jnp.sum(probs, axis=0, keepdims=True))
        probs_b = probs.astype(BF16)
        o_blk = dot_nn(v_t[:, :stop], probs_b).astype(BF16)
        d_probs = dot_nt(v_blk, do_blk)
        delta = jnp.sum(probs * d_probs, axis=0, keepdims=True)
        d_scores = (probs * (d_probs - delta)).astype(BF16)
        dq_blk = dot_nn(k_t[:, :stop], d_scores) * score_scale
        dk_new, dv_new = dot_nn(d_scores, q_blk), dot_nn(probs_b, do_blk)
        if stop == full:
            k_acc[...], v_acc[...] = dk_new, dv_new
        else:
            k_acc[0:stop, :] += dk_new
            v_acc[0:stop, :] += dv_new
        for h in range(heads):
            o_blocks[h].append(o_blk[:, h * block:(h + 1) * block])
            dq_blocks[h].append(dq_blk[:, h * block:(h + 1) * block].T)
    for h in range(heads):
        o_t = jnp.concatenate(o_blocks[h][::-1], axis=1)
        put(h * dim, o_t.T)
        o_acc[h * dim:(h + 1) * dim, :] += dot_nn(o_t, dy_rows)
        _, unit, scale = q_parts[h]
        dq, weight_grad = head_backward(jnp.concatenate(dq_blocks[h][::-1], axis=0), unit, scale, q_weights[h], cos_t, sin_t)
        put(width + h * dim, dq)
        qkv_acc[h * dim:(h + 1) * dim, :] += dot_nn(dq.T, n_rows)
        wn_ref[h:h + 1, :] += weight_grad
    dk, weight_grad = head_backward(k_acc[...] * score_scale, k_unit, k_scale, k_weight, cos_t, sin_t)
    wn_ref[heads:heads + 1, :] += weight_grad
    dv = v_acc[...].astype(BF16)
    put(2 * width, dk)
    put(2 * width + dim, dv)
    qkv_acc[width:width + dim, :] += dot_nn(dk.T, n_rows)
    qkv_acc[width + dim:width + 2 * dim, :] += dot_nn(dv.T, n_rows)


def front_kernel(n_ref, dy_ref, wg_ref, wu_ref, wd_ref, rope_ref, wq_ref, wk_ref, wv_ref, wo_ref, qn_ref, kn_ref,
                 m_ref, dn_ref, gn_ref, gdy_ref, mix_ref, wn_ref, packed_ref,
                 n_all, dy_all, rope_all, m_acc, k_acc, v_acc, qkv_acc, o_acc, send_sem, recv_sem, rope_send, rope_recv, out_sem, *, count, blocks, heads, dim):
    step = pl.program_id(0)
    me = lax.axis_index('sp')
    right, left, across, partner = lax.rem(me + 2, count), lax.rem(me + count - 2, count), lax.rem(me + 4, count), me + 1 - 2 * lax.rem(me, 2)
    other = lambda device: device + 1 - 2 * lax.rem(device, 2)
    batch, _, piece, model = n_all.shape

    def send(seq, index, src, into, slot, target):
        return pltpu.make_async_remote_copy(src_ref=src, dst_ref=into.at[seq, slot], send_sem=send_sem.at[seq, index], recv_sem=recv_sem.at[seq, index],
                                            device_id={'sp': target}, device_id_type=MESH)

    def forward(seq, index, ref, slot, target):
        return send(seq, index, ref.at[seq, slot], ref, slot, target)

    def own(seq):
        rows = pl.ds(pl.multiple_of(seq * piece, piece), piece)
        n, dy = n_ref.at[rows], dy_ref.at[rows]
        return [send(seq, 0, dy, dy_all, me, right), send(seq, 2, n, n_all, me, left), send(seq, 1, n, n_all, me, right),
                send(seq, 3, dy, dy_all, me, left), send(seq, 4, n, n_all, me, partner), send(seq, 5, dy, dy_all, me, partner)]

    def early(seq):
        return [forward(seq, 6, dy_all, left, right), forward(seq, 8, dy_all, left, partner), forward(seq, 7, n_all, right, left), forward(seq, 9, n_all, right, partner)]

    def late(seq):
        return [forward(seq, 10, n_all, left, partner), forward(seq, 11, dy_all, right, partner),
                forward(seq, 12, dy_all, across, partner), forward(seq, 13, n_all, across, partner)]

    def arrived(seq, index, ref, slot):
        send(seq, index, ref.at[seq, slot], ref, slot, partner).wait_recv()

    def start_own(seq):
        for copy in own(seq):
            copy.start()

    def pass_early(seq):
        copies = early(seq)
        arrived(seq, 0, dy_all, left)
        copies[0].start()
        copies[1].start()
        arrived(seq, 2, n_all, right)
        copies[2].start()
        copies[3].start()

    def pass_late(seq):
        for copy, (index, ref, slot) in zip(late(seq), ((1, n_all, left), (3, dy_all, right), (6, dy_all, across), (7, n_all, across))):
            arrived(seq, index, ref, slot)
            copy.start()

    def complete(seq):
        for index, ref, slot in ((4, n_all, partner), (5, dy_all, partner), (8, dy_all, other(left)), (9, n_all, other(right)),
                                 (10, n_all, other(left)), (11, dy_all, other(right)), (12, dy_all, other(across)), (13, n_all, other(across))):
            arrived(seq, index, ref, slot)

    def tables():
        return [pltpu.make_async_remote_copy(src_ref=rope_ref, dst_ref=rope_all.at[me], send_sem=rope_send.at[i], recv_sem=rope_recv.at[i],
                                             device_id={'sp': device}, device_id_type=MESH) for i, device in enumerate(other_devices(count))]

    def to_memory(seq):
        return [pltpu.make_async_copy(n_all.at[seq], gn_ref.at[seq], out_sem.at[seq, 0]), pltpu.make_async_copy(dy_all.at[seq], gdy_ref.at[seq], out_sem.at[seq, 1])]

    @pl.when(step == 0)
    def _():
        meet(count)
        start_own(0)
        for copy in tables():
            copy.start()
        start_own(1)
        for seq in range(batch):
            rows = slice(seq * piece, (seq + 1) * piece)
            n_all[seq, pl.ds(me, 1)] = n_ref[rows, :][None]
            dy_all[seq, pl.ds(me, 1)] = dy_ref[rows, :][None]
        rope_all[pl.ds(me, 1)] = rope_ref[...][None]
        wn_ref[...] = jnp.zeros_like(wn_ref)
        qkv_acc[...] = jnp.zeros_like(qkv_acc)
        o_acc[...] = jnp.zeros_like(o_acc)

    @pl.when(step == 2)
    def _():
        pass_early(0)

    @pl.when(step == 3)
    def _():
        start_own(2)

    @pl.when(step == blocks - 1)
    def _():
        pass_early(1)
        pass_late(0)

    @pl.when(step < blocks)
    def _():
        n, dy = n_ref[...], dy_ref[...]
        wg, wu, wd = wg_ref[...], wu_ref[...], wd_ref[...]
        hidden, d_gate, d_up = swiglu_both(dot_nn(n, wg), dot_nn(n, wu), dot_nt(dy, wd))
        m_new = dot_nn(hidden, wd)
        dn_new = dot_nt(d_gate, wg) + dot_nt(d_up, wu)

        @pl.when(step == 0)
        def _():
            m_acc[...] = m_new
            dn_ref[...] = dn_new

        @pl.when(step > 0)
        def _():
            m_acc[...] += m_new
            dn_ref[...] += dn_new

        @pl.when(step == blocks - 1)
        def _():
            m_ref[...] = m_acc[...].astype(BF16)

    @pl.when(step == blocks)
    def _():
        for copy in tables():
            copy.wait()

    @pl.when(step >= blocks)
    def _():
        seq = step - blocks

        @pl.when(seq + 3 < batch)
        def _():
            start_own(seq + 3)

        @pl.when(seq + 1 < batch)
        def _():
            pass_late(seq + 1)

        complete(seq)
        for copy in to_memory(seq):
            copy.start()
        full = count * piece
        one_sequence(me, n_all[seq].reshape(full, model), dy_all[seq].reshape(full, model), rope_all[:, 0].reshape(full, dim), rope_all[:, 1].reshape(full, dim),
                     wq_ref, wk_ref, wv_ref, wo_ref, qn_ref, kn_ref, mix_ref, wn_ref, k_acc, v_acc, qkv_acc, o_acc, heads, dim, min(128, full))

        @pl.when(seq + 2 < batch)
        def _():
            pass_early(seq + 2)

    @pl.when(step == pl.num_programs(0) - 1)
    def _():
        qkv_size = qkv_acc.shape[0]
        size = o_acc.shape[0]
        packed_ref[:, :qkv_size] = qkv_acc[...].T.astype(BF16)
        for i in range(model // size):
            packed_ref[i * size:(i + 1) * size, qkv_size:] = o_acc[:, i * size:(i + 1) * size].astype(BF16)

        @pl.loop(0, batch)
        def _(seq):
            for copy in own(seq) + early(seq) + late(seq):
                copy.wait_send()
            for copy in to_memory(seq):
                copy.wait()


def front(n, dy, w_gate, w_up, w_down, rope, w_q, w_k, w_v, w_o, q_norm, k_norm, count, piece, block):
    rows, model = n.shape
    ffn = w_gate.shape[1]
    num_heads, dim = q_norm.shape
    heads = num_heads // k_norm.shape[0]
    batch = rows // piece
    blocks = ffn // block
    width = (2 * heads + 2) * dim
    one = pl.Buffered(1)
    whole = lambda shape: pl.BlockSpec(shape, lambda i: (0,) * len(shape), pipeline_mode=one)
    cols = pl.BlockSpec((model, block), lambda i: (0, jnp.minimum(i, blocks - 1)))
    mine = lambda size: pl.BlockSpec((model, size), lambda i: (0, lax.axis_index('sp')), pipeline_mode=one)
    away = pl.BlockSpec(memory_space=pl.ANY)
    dma = pltpu.SemaphoreType.DMA
    vmem = pltpu.VMEM
    shape = jax.ShapeDtypeStruct
    return pl.pallas_call(
        functools.partial(front_kernel, count=count, blocks=blocks, heads=heads, dim=dim),
        grid=(blocks + batch,),
        in_specs=[whole((rows, model)), whole((rows, model)), cols, cols, pl.BlockSpec((block, model), lambda i: (jnp.minimum(i, blocks - 1), 0)), whole(rope.shape),
                  mine(heads * dim), mine(dim), mine(dim), pl.BlockSpec((heads * dim, model), lambda i: (lax.axis_index('sp'), 0), pipeline_mode=one),
                  whole(q_norm.shape), whole(k_norm.shape)],
        out_specs=[whole((rows, model)), whole((rows, model)), away, away,
                   pl.BlockSpec((count, 1, piece, width), lambda i: (0, jnp.maximum(i - blocks, 0), 0, 0)), whole((8, dim)), whole((model, width))],
        out_shape=[shape((rows, model), BF16), shape((rows, model), F32), shape((batch, count, piece, model), BF16), shape((batch, count, piece, model), BF16),
                   shape((count, batch, piece, width), BF16), shape((8, dim), F32), shape((model, width), BF16)],
        scratch_shapes=[vmem((batch, count, piece, model), BF16), vmem((batch, count, piece, model), BF16), vmem((count,) + rope.shape, F32), vmem((rows, model), F32),
                        vmem((count * piece, dim), F32), vmem((count * piece, dim), F32), vmem(((heads + 2) * dim, model), F32), vmem((heads * dim, model), F32),
                        dma((batch, 14)), dma((batch, 14)), dma((count - 1,)), dma((count - 1,)), dma((batch, 2))],
        compiler_params=pltpu.CompilerParams(vmem_limit_bytes=62 * 2 ** 20, collective_id=0, has_side_effects=True),
        cost_estimate=pl.CostEstimate(flops=12 * rows * model * ffn + 8 * batch * count * piece * model * width, bytes_accessed=6 * model * ffn, transcendentals=0),
    )(n, dy, w_gate, w_up, w_down, rope, w_q, w_k, w_v, w_o, q_norm, k_norm)


def norm_kernel(x_ref, gain_ref, n_ref):
    x = x_ref[...].astype(F32)
    centered = x - jnp.mean(x, axis=-1, keepdims=True)
    scale = lax.rsqrt(jnp.mean(centered * centered, axis=-1, keepdims=True) + NORM_EPS)
    n_ref[...] = (centered * scale * gain_ref[...]).astype(BF16)


def input_norm(x, gain):
    rows, model = x.shape
    tile = rows // 4
    return pl.pallas_call(
        norm_kernel,
        grid=(rows // tile,),
        in_specs=[pl.BlockSpec((tile, model), lambda i: (i, 0)), pl.BlockSpec((1, model), lambda i: (0, 0))],
        out_specs=pl.BlockSpec((tile, model), lambda i: (i, 0)),
        out_shape=jax.ShapeDtypeStruct((rows, model), BF16),
        cost_estimate=pl.CostEstimate(flops=8 * rows * model, bytes_accessed=4 * rows * model, transcendentals=0),
    )(x, gain)


def finish_kernel(core_ref, mix_ref, x_ref, dy_ref, m_ref, dn_ref, gain_ref, wq_ref, wk_ref, wv_ref, wo_ref, gg_ref, gu_ref, gd_ref, pg_ref, pu_ref, pd_ref,
                  y_ref, dx_ref, gain_grad_ref, fg_ref, fu_ref, fd_ref, a_acc, d_acc, col_buf, row_buf, in_sem, out_sem, *, parts):
    step = pl.program_id(0)
    steps = pl.num_programs(0)
    o_size, k_size = parts
    share = gg_ref.shape[1]
    slots, _, col_rows, _ = col_buf.shape
    row_rows = row_buf.shape[2]
    mine, theirs = pl.multiple_of(core_ref[0] * share, share), pl.multiple_of((1 - core_ref[0]) * share, share)

    def fetches(at):
        slot = lax.rem(at, slots)
        cols = pl.ds(pl.multiple_of(at * col_rows, col_rows), col_rows)
        rows = pl.ds(pl.multiple_of(at * row_rows, row_rows), row_rows)
        pairs = [(ref.at[cols], col_buf.at[slot, i]) for i, ref in enumerate((gg_ref, gu_ref, pg_ref, pu_ref))]
        pairs += [(ref.at[rows], row_buf.at[slot, i]) for i, ref in enumerate((gd_ref, pd_ref))]
        return [pltpu.make_async_copy(src, dst, in_sem.at[slot, i]) for i, (src, dst) in enumerate(pairs)]

    def places(at):
        slot = lax.rem(at, slots)
        cols = pl.ds(pl.multiple_of(at * col_rows, col_rows), col_rows)
        pairs = [(col_buf.at[slot, i], ref.at[cols, pl.ds(start, share)]) for i, (ref, start) in enumerate(((fg_ref, mine), (fu_ref, mine), (fg_ref, theirs), (fu_ref, theirs)))]
        pairs += [(row_buf.at[slot, i], fd_ref.at[pl.ds(pl.multiple_of(start + at * row_rows, row_rows), row_rows)]) for i, start in enumerate((mine, theirs))]
        return [pltpu.make_async_copy(src, dst, out_sem.at[slot, i]) for i, (src, dst) in enumerate(pairs)]

    @pl.when(step == 0)
    def _():
        for copy in fetches(0):
            copy.start()

    @pl.when(step > 1)
    def _():
        for copy in places(step - 2):
            copy.wait()

    @pl.when(step < steps - 1)
    def _():
        for copy in fetches(step + 1):
            copy.start()

    mix = mix_ref[0]
    a_new = dot_nn(mix[:, :o_size], wo_ref[...])
    d_new = dot_nt(mix[:, o_size:2 * o_size], wq_ref[...])
    d_new += dot_nt(mix[:, 2 * o_size:2 * o_size + k_size], wk_ref[...]) + dot_nt(mix[:, 2 * o_size + k_size:], wv_ref[...])

    @pl.when(step == 0)
    def _():
        a_acc[...] = a_new
        d_acc[...] = d_new + dn_ref[...]

    @pl.when(step > 0)
    def _():
        a_acc[...] += a_new
        d_acc[...] += d_new

    for copy in fetches(step):
        copy.wait()
    for copy in places(step):
        copy.start()

    @pl.when(step == steps - 1)
    def _():
        x = x_ref[...].astype(F32)
        y_ref[...] = (x + a_acc[...].astype(BF16).astype(F32) + m_ref[...].astype(F32)).astype(BF16)
        centered = x - jnp.mean(x, axis=-1, keepdims=True)
        scale = lax.rsqrt(jnp.mean(centered * centered, axis=-1, keepdims=True) + NORM_EPS)
        unit = centered * scale
        grad = d_acc[...].astype(BF16).astype(F32)
        gain_grad = jnp.sum(grad * unit, axis=0, keepdims=True)
        rows, lanes = gain_grad_ref.shape
        for i in range(rows):
            gain_grad_ref[i:i + 1, :] = gain_grad[:, i * lanes:(i + 1) * lanes]
        grad = grad * gain_ref[...]
        along = jnp.mean(grad * unit, axis=-1, keepdims=True)
        grad = scale * (grad - jnp.mean(grad, axis=-1, keepdims=True) - unit * along)
        dx_ref[...] = (dy_ref[...].astype(F32) + grad).astype(BF16)
        for copy in places(step - 1) + places(step):
            copy.wait()


def finish(core, mix, x, dy, mlp_out, d_norm, gain, w_q, w_k, w_v, w_o, own_grads, partner_grads, o_size, k_size):
    rows, model = x.shape
    pieces, _, width = mix.shape
    share = own_grads[0].shape[1]
    whole = pl.BlockSpec((rows, model), lambda i, c: (0, 0))
    row = pl.BlockSpec((1, model), lambda i, c: (0, 0))
    gain_shape = (model // k_size, k_size)
    cols = lambda size: pl.BlockSpec((model, size), lambda i, c: (0, i))
    away = pl.BlockSpec(memory_space=pl.ANY)
    bf16 = lambda *shape: jax.ShapeDtypeStruct(shape, BF16)
    return pl.pallas_call(
        functools.partial(finish_kernel, parts=(o_size, k_size)),
        grid_spec=pltpu.PrefetchScalarGridSpec(
            num_scalar_prefetch=1,
            grid=(pieces,),
            in_specs=[pl.BlockSpec((1, rows, width), lambda i, c: (i, 0, 0))] + [whole] * 4
            + [row, cols(o_size), cols(k_size), cols(k_size), pl.BlockSpec((o_size, model), lambda i, c: (i, 0))] + [away] * 6,
            out_specs=[whole, whole, pl.BlockSpec(gain_shape, lambda i, c: (0, 0))] + [away] * 3,
            scratch_shapes=[pltpu.VMEM((rows, model), F32), pltpu.VMEM((rows, model), F32),
                            pltpu.VMEM((3, 4, model // pieces, share), BF16), pltpu.VMEM((3, 2, share // pieces, model), BF16),
                            pltpu.SemaphoreType.DMA((3, 6)), pltpu.SemaphoreType.DMA((3, 6))],
        ),
        out_shape=[bf16(rows, model), bf16(rows, model), jax.ShapeDtypeStruct(gain_shape, F32)]
        + [bf16(model, 2 * share), bf16(model, 2 * share), bf16(2 * share, model)],
        compiler_params=pltpu.CompilerParams(vmem_limit_bytes=56 * 2 ** 20),
        cost_estimate=pl.CostEstimate(flops=2 * pieces * rows * width * model, bytes_accessed=14 * rows * model + 2 * pieces * width * (rows + model), transcendentals=0),
    )(core, mix, x, dy, mlp_out, d_norm, gain, w_q, w_k, w_v, w_o, *own_grads, *partner_grads)


def place_kernel(packed_ref, fq_ref, fk_ref, fv_ref, fo_ref, buf, in_sem, out_sem, *, o_size, k_size):
    count, model, _ = packed_ref.shape
    fetch = lambda at: pltpu.make_async_copy(packed_ref.at[at], buf.at[at], in_sem.at[at])

    def places(at):
        part = buf.at[at]
        pairs = [(part.at[:, pl.ds(0, o_size)], fq_ref.at[:, pl.ds(at * o_size, o_size)]), (part.at[:, pl.ds(o_size, k_size)], fk_ref.at[:, pl.ds(at * k_size, k_size)]),
                 (part.at[:, pl.ds(o_size + k_size, k_size)], fv_ref.at[:, pl.ds(at * k_size, k_size)])]
        pairs += [(part.at[pl.ds(i * o_size, o_size), pl.ds(o_size + 2 * k_size, o_size)], fo_ref.at[pl.ds(at * o_size, o_size), pl.ds(i * o_size, o_size)])
                  for i in range(model // o_size)]
        return [pltpu.make_async_copy(src, dst, out_sem.at[at, i]) for i, (src, dst) in enumerate(pairs)]

    for at in range(count):
        fetch(at).start()
    for at in range(count):
        fetch(at).wait()
        for copy in places(at):
            copy.start()
    for at in range(count):
        for copy in places(at):
            copy.wait()


def place(packed, weights, o_size, k_size):
    count, model, _ = packed.shape
    away = pl.BlockSpec(memory_space=pl.ANY)
    return pl.pallas_call(
        functools.partial(place_kernel, o_size=o_size, k_size=k_size),
        in_specs=[away],
        out_specs=[away] * 4,
        out_shape=[jax.ShapeDtypeStruct(weight.shape, BF16) for weight in weights],
        scratch_shapes=[pltpu.VMEM(packed.shape, BF16), pltpu.SemaphoreType.DMA((count,)), pltpu.SemaphoreType.DMA((count, 3 + model // o_size))],
        compiler_params=pltpu.CompilerParams(vmem_limit_bytes=40 * 2 ** 20),
        cost_estimate=pl.CostEstimate(flops=2 ** 20, bytes_accessed=4 * packed.size, transcendentals=0),
    )(packed)


def share_kernel(gain_ref, norm_ref, gain_out, q_out, k_out, parts, send_sem, recv_sem, *, count, heads):
    me = lax.axis_index('sp')
    rows = gain_ref.shape[0]
    meet(count)
    copies = [pltpu.make_async_remote_copy(src_ref=src, dst_ref=parts.at[me, pl.ds(j * rows, rows)], send_sem=send_sem.at[i, j], recv_sem=recv_sem.at[i, j],
                                           device_id={'sp': device}, device_id_type=MESH)
              for i, device in enumerate(other_devices(count)) for j, src in enumerate((gain_ref, norm_ref))]
    for copy in copies:
        copy.start()
    parts[pl.ds(me, 1), :rows] = gain_ref[...][None]
    parts[pl.ds(me, 1), rows:] = norm_ref[...][None]
    for copy in copies:
        copy.wait()
    gain_out[...] = jnp.sum(parts[:, :rows], axis=0)
    for device in range(count):
        q_out[device * heads:(device + 1) * heads, :] = parts[device, rows:rows + heads, :]
        k_out[device:device + 1, :] = parts[device, rows + heads:rows + heads + 1, :]


def share_small(gain, norms, q_norm, k_norm, count):
    vmem = pl.BlockSpec(memory_space=pltpu.VMEM)
    heads = q_norm.shape[0] // k_norm.shape[0]
    dma = pltpu.SemaphoreType.DMA((count - 1, 2))
    return pl.pallas_call(
        functools.partial(share_kernel, count=count, heads=heads),
        in_specs=[vmem] * 2,
        out_specs=[vmem] * 3,
        out_shape=[jax.ShapeDtypeStruct(part.shape, F32) for part in (gain, q_norm, k_norm)],
        scratch_shapes=[pltpu.VMEM((count, 2 * gain.shape[0], gain.shape[1]), F32), dma, dma],
        compiler_params=pltpu.CompilerParams(collective_id=2, has_side_effects=True),
    )(gain, norms)


def solution(mesh):
    n_sp = mesh.shape['sp']
    seq_spec = P('dp', 'sp', None)
    grad_spec = P('dp', None)

    def layer_step(x_in, grad_y, positions, w_q, w_k, w_v, w_o, w_gate, w_up, w_down, norm_gain, q_norm, k_norm):
        batch, piece, model = x_in.shape
        num_heads, dim = q_norm.shape
        heads = num_heads // k_norm.shape[0]
        ffn = w_gate.shape[1]
        tokens = batch * piece
        me = lax.axis_index('sp')
        gain_row = norm_gain.reshape(1, model)
        x_rows, dy_own = x_in.reshape(tokens, model), grad_y.reshape(tokens, model)
        n_own = input_norm(x_rows, gain_row)

        inv_freq = ROPE_THETA ** (-(jnp.arange(dim // 2, dtype=F32) * 2.0) / dim)
        angles = jnp.repeat(positions.astype(F32)[:, None] * inv_freq[None, :], 2, axis=1)
        sign = jnp.where(jnp.arange(dim) % 2 == 0, -1.0, 1.0).astype(F32)
        rope_own = jnp.stack([jnp.cos(angles), jnp.sin(angles) * sign[None, :]])

        mlp_out, d_norm, n_all, dy_all, mix, norm_grads, packed = front(n_own, dy_own, w_gate, w_up, w_down, rope_own, w_q, w_k, w_v, w_o, q_norm, k_norm,
                                                                        n_sp, piece, ffn // 6)
        packed = lax.all_gather(packed, 'sp', axis=0, tiled=False)

        by_tile = lambda part: part.reshape(n_sp, -1, part.shape[-1])
        *grads, mix = all_mlp([(by_tile(n_all), 0)], [(by_tile(dy_all), 0)], w_gate, w_up, w_down, by_tile(mix), ffn // 6)

        y_out, grad_x, grad_gain, full_gate, full_up, full_down = finish((me % 2).reshape(1), mix, x_rows, dy_own, mlp_out, d_norm, gain_row, w_q, w_k, w_v, w_o,
                                                                         grads[:3], grads[3:], heads * dim, dim)
        full_gain, full_qn, full_kn = share_small(grad_gain, norm_grads, q_norm, k_norm, n_sp)
        packed, full_gain = lax.optimization_barrier((packed, full_gain))
        full_q, full_k, full_v, full_o = place(packed, (w_q, w_k, w_v, w_o), heads * dim, dim)
        return (y_out.reshape(x_in.shape), grad_x.reshape(x_in.shape), full_q, full_k, full_v, full_o, full_gate, full_up, full_down,
                full_gain.reshape(model), full_qn, full_kn)

    in_specs = (seq_spec, seq_spec, P(('dp', 'sp'))) + (P(),) * 10
    out_specs = (seq_spec, seq_spec) + (grad_spec,) * 7 + (P('dp'), grad_spec, grad_spec)
    return jax.shard_map(layer_step, mesh=mesh, in_specs=in_specs, out_specs=out_specs, check_vma=False)
```

time: 333 us -> 326 us (0.979)
  starting transfers between devices: 4.96 us -> 0.06 us
    pallas_call x1, Pallas kernels: 131 us -> 142 us  [all_mlp(): pl.pallas_call(functools.partial(all_mlp_kernel, chunks=len(n_chunks), bl...]
    pallas_call x5 -> x4, Pallas kernels: 166 us -> 157 us  [the longest x1 120 us: front(): pl.pallas_call(functools.partial(front_kernel, count=count, blocks=blocks...]
    all_to_all x1 -> x0, starting transfers between devices: 4.83 us -> none  [layer_step(): mix_0 = lax.all_to_all(mix_0, 'sp', 0, 0, tiled=True)]
    unnamed x8 -> x11, local copies, waits for them, and re-layouts: 3 us -> 6.37 us
  transfers between devices with their start and end apart: 3 -> 1, of which waited for: 1 -> 0; matrix products, arithmetic and copies ran while one was open for 0% -> 0% of each run, Pallas kernels for 51% -> 53%
where the time goes in v1:
time: 326 us; the launch traced here: 325 us
  Pallas kernels  303 us (93%)
  between operations  14.2 us (4%)
  local copies, waits for them, and re-layouts  6.56 us (2%)
    pallas_call x1, Pallas kernels, all_mlp(): pl.pallas_call(functools.partial(all_mlp_kernel, chunks=len(n_chunks), bl...  142 us
    pallas_call x1, Pallas kernels, front(): pl.pallas_call(functools.partial(front_kernel, count=count, blocks=blocks...  120 us
    pallas_call x1, Pallas kernels, finish(): pl.pallas_call(functools.partial(finish_kernel, parts=(o_size, k_size)),...  24.5 us
    pallas_call x1, Pallas kernels, share_small(): pl.pallas_call(functools.partial(share_kernel, count=count, heads=heads),...  6.85 us
  transfers between devices with their start and end apart: 1, of which 0 were waited for; matrix products, arithmetic and copies ran while one was open for 0% of the time, Pallas kernels for 53%

profile of v1, /device:TPU:81, one launch (start us, length us, event | category | flops | bytes accessed | tf_op | source)
XLA Modules:
  0.0 325.4 jit_solution(4714036815774774826)
XLA Ops:
  7.2 0.1 all-gather.3.cloned.1.call-start
  7.3 0.7 convert_element_type.3
  7.9 0.2 multiply_cosine_fusion
  8.2 0.1 copy.25
  8.3 0.1 copy.26
  8.4 3.9 %shard_map.220.n_ref = bf16[512,1024]{1,0:T(8,128)(2,1)} custom-call(bf16[512,1024]{1,0:T(8,128)(2,1)} %bitcast.14, f32[1,1024]{1,0:T(1,128)} %bitcast.20), custom_call_target="tpu_custom_call" | custom-call | flops 4194304 | bytes 2097152 | tf_op jit(solution)/shard_map/pallas_call | solution.py:442
  12.2 0.6 pad_maximum_fusion.rope_ref
  12.9 120.0 %shard_map.221 = (bf16[512,1024]{1,0:T(8,128)(2,1)}, f32[512,1024]{1,0:T(8,128)}, bf16[8,8,64,1024]{3,2,1,0:T(8,128)(2,1)}, bf16[8,8,64,1024]{3,2,1,0:T(8,128)(2...) custom-call(bf16[512,1024]{1,0:T(8,128)(2,1)} %shard_map.220.n_ref, ...), custom_call_target="tpu_custom_call" | custom-call | flops 45097156608 | bytes 18874368 | tf_op jit(solution)/shard_map/pallas_call | solution.py:414
  132.9 0.1 all-gather.3.cloned.1.call-update
  133.0 141.9 %shard_map.222 = (bf16[1024,1536]{1,0:T(8,128)(2,1)}, bf16[1024,1536]{1,0:T(8,128)(2,1)}, bf16[1536,1024]{1,0:T(8,128)(2,1)}, bf16[1024,1536]{1,0:T(8,128)(2,1)}...) custom-call(bf16[8,512,1024]{2,1,0:T(8,128)(2,1)} %bitcast.25, ...), custom_call_target="tpu_custom_call" | custom-call | flops 77309411328 | bytes 35651584 | tf_op jit(solution)/shard_map/pallas_call | solution.py:137
  274.9 24.5 %shard_map.223 = (bf16[512,1024]{1,0:T(8,128)(2,1)}, bf16[512,1024]{1,0:T(8,128)(2,1)}, f32[8,128]{1,0:T(8,128)}, bf16[1024,3072]{1,0:T(8,128)(2,1)}, bf16[1024,...) custom-call(s32[1]{0:T(128)} %bitcast.core_ref, bf16[8,512,768]{2,1,0:T(8,128)(2,1)} %get-tuple-element.44.mix_ref, ...), custom_call_target="tpu_custom_call" | custom-call | flops 6442450944 | bytes 26214400 | tf_op jit(solution)/shard_map/pallas_call | solution.py:542
  299.4 6.8 %shard_map.224 = (f32[8,128]{1,0:T(8,128)}, f32[16,128]{1,0:T(8,128)}, f32[8,128]{1,0:T(8,128)}) custom-call(f32[8,128]{1,0:T(8,128)} %get-tuple-element.56.gain_ref, f32[8,128]{1,0:T(8,128)} %get-tuple-element.57.norm_ref), custom_call_target="tpu_custom_call" | custom-call | tf_op jit(solution)/shard_map/pallas_call | solution.py:621
  306.3 0.0 all-gather.3.cloned.1.call-done
  306.3 0.0 copy-start
  306.3 4.6 %copy-done = bf16[8192,768]{1,0:T(8,128)(2,1)S(1)} copy-done((bf16[8192,768]{1,0:T(8,128)(2,1)S(1)}, bf16[8192,768]{1,0:T(8,128)(2,1)}, u32[]{:S(2)}) %copy-start) | copy-done | bytes 12582936
  310.9 0.0 copy-start.3
  310.9 0.0 copy-start.1
  310.9 0.0 copy-start.2
  310.9 5.9 %shard_map.225 = (bf16[1024,2048]{1,0:T(8,128)(2,1)}, bf16[1024,1024]{1,0:T(8,128)(2,1)}, bf16[1024,1024]{1,0:T(8,128)(2,1)}, bf16[2048,1024]{1,0:T(8,128)(2,1)}) custom-call(bf16[8,1024,768]{2,1,0:T(8,128)(2,1)S(1)} %bitcast.13), custom_call_target="tpu_custom_call" | custom-call | flops 1048576 | bytes 25165824 | tf_op jit(solution)/shard_map/pallas_call | solution.py:587
  316.8 0.0 copy-done.3
  316.8 0.6 copy.30
  317.4 0.0 copy-done.1
  317.4 0.6 copy.31
  318.0 0.0 copy-done.2
  318.0 0.6 copy.32
  (5 shorter events, 0.1 us)
Async XLA Ops:
  7.2 299.1 %all-gather.3.cloned.1.call-start = ((), (), s32[]{:S(2)}) async-start(), calls=%async_computation | async-start | bytes 14155776 | tf_op jit(solution)/shard_map/all_gather | solution.py:654
  306.3 4.6 %copy-start = (bf16[8192,768]{1,0:T(8,128)(2,1)S(1)}, bf16[8192,768]{1,0:T(8,128)(2,1)}, u32[]{:S(2)}) copy-start(bf16[8192,768]{1,0:T(8,128)(2,1)} %all-gather.3.cloned.1.call-done) | copy-start | bytes 37748740
  310.9 5.9 %copy-start.3 = (f32[8,128]{1,0:T(8,128)S(1)}, f32[8,128]{1,0:T(8,128)}, u32[]{:S(2)}) copy-start(f32[8,128]{1,0:T(8,128)} %get-tuple-element.67) | copy-start | bytes 12292
  310.9 6.5 %copy-start.1 = (f32[16,128]{1,0:T(8,128)S(1)}, f32[16,128]{1,0:T(8,128)}, u32[]{:S(2)}) copy-start(f32[16,128]{1,0:T(8,128)} %get-tuple-element.94) | copy-start | bytes 24580
  310.9 7.1 %copy-start.2 = (f32[8,128]{1,0:T(8,128)S(1)}, f32[8,128]{1,0:T(8,128)}, u32[]{:S(2)}) copy-start(f32[8,128]{1,0:T(8,128)} %get-tuple-element.95) | copy-start | bytes 12292
Sparse Core Ops, SparseCore 0:
  133.1 135.2 all-gather.2

commit v2 on v1

--- a/solution.py
+++ b/solution.py
@@ -42,19 +42,25 @@
     pl.semaphore_wait(barrier, count - 1)
 
 
-def all_mlp_kernel(*refs, chunks, block, count):
-    n_refs, dy_refs = refs[:chunks], refs[chunks:2 * chunks]
-    (wg_ref, wu_ref, wd_ref, mix_ref, gg_ref, gu_ref, gd_ref, pg_ref, pu_ref, pd_ref, swap_ref,
-     n_all, dy_all, n_t, dy_t, acc_g, acc_u, acc_d, swap_send, swap_recv, half_send, half_recv, own_sem) = refs[2 * chunks:]
+def all_mlp_kernel(n_ref, dy_ref, wg_ref, wu_ref, wd_ref, mix_ref, qk_ref, vo_ref, gg_ref, gu_ref, gd_ref, pg_ref, pu_ref, pd_ref, swap_ref, qk_all, vo_all,
+                   n_t, dy_t, acc_g, acc_u, acc_d, swap_send, swap_recv, half_send, half_recv, ring_send, ring_recv, own_sem, *, block, count):
     step = pl.program_id(0)
     last = pl.num_programs(0) - 1
     share = wg_ref.shape[1]
     me = lax.axis_index('sp')
-    partner = me + 1 - 2 * lax.rem(me, 2)
-
-    def swaps():
-        return [pltpu.make_async_remote_copy(src_ref=mix_ref.at[device], dst_ref=swap_ref.at[me], send_sem=swap_send.at[i], recv_sem=swap_recv.at[i],
-                                             device_id={'sp': device}, device_id_type=MESH) for i, device in enumerate(other_devices(count))]
+    right, left, across, partner = lax.rem(me + 2, count), lax.rem(me + count - 2, count), lax.rem(me + 4, count), me + 1 - 2 * lax.rem(me, 2)
+    other = lambda device: device + 1 - 2 * lax.rem(device, 2)
+
+    def swaps(shifts):
+        copies = []
+        for shift in shifts:
+            device = lax.rem(me + shift, count)
+            copies.append(pltpu.make_async_remote_copy(src_ref=mix_ref.at[device], dst_ref=swap_ref.at[me], send_sem=swap_send.at[shift - 1], recv_sem=swap_recv.at[shift - 1],
+                                                       device_id={'sp': device}, device_id_type=MESH))
+        return copies
+
+    near = [1, count - 1, 2, count - 2]
+    far = [shift for shift in range(3, count - 2)]
 
     def halves(i):
         cols = pl.ds(i * block, block)
@@ -62,31 +68,46 @@
                                              device_id={'sp': partner}, device_id_type=MESH)
                 for j, (src, dst, index) in enumerate(((gg_ref, pg_ref, (slice(None), cols)), (gu_ref, pu_ref, (slice(None), cols)), (gd_ref, pd_ref, (cols,))))]
 
-    keep = lambda: pltpu.make_async_copy(mix_ref.at[me], swap_ref.at[me], own_sem)
+    def send(index, src, into, slot, target):
+        return pltpu.make_async_remote_copy(src_ref=src, dst_ref=into.at[slot], send_sem=ring_send.at[index], recv_sem=ring_recv.at[index],
+                                            device_id={'sp': target}, device_id_type=MESH)
+
+    def forward(index, ref, slot, target):
+        return send(index, ref.at[slot], ref, slot, target)
+
+    def arrived(index, ref, slot):
+        send(index, ref.at[slot], ref, slot, partner).wait_recv()
+
+    own = lambda: [send(0, vo_ref, vo_all, me, right), send(2, qk_ref, qk_all, me, left), send(1, qk_ref, qk_all, me, right),
+                   send(3, vo_ref, vo_all, me, left), send(4, qk_ref, qk_all, me, partner), send(5, vo_ref, vo_all, me, partner)]
+    early = lambda: [forward(6, vo_all, left, right), forward(7, qk_all, right, left), forward(8, vo_all, left, partner), forward(9, qk_all, right, partner)]
+    late = lambda: [forward(10, qk_all, left, partner), forward(11, vo_all, right, partner), forward(12, vo_all, across, partner), forward(13, qk_all, across, partner)]
+    keep = lambda: [pltpu.make_async_copy(mix_ref.at[me], swap_ref.at[me], own_sem.at[0]), pltpu.make_async_copy(qk_ref, qk_all.at[me], own_sem.at[1]),
+                    pltpu.make_async_copy(vo_ref, vo_all.at[me], own_sem.at[2])]
 
     @pl.when(step == 0)
     def _():
         meet(count)
-        keep().start()
-        for copy in swaps():
+        for copy in own() + swaps(near) + keep():
             copy.start()
         acc_g[...] = jnp.zeros_like(acc_g)
         acc_u[...] = jnp.zeros_like(acc_u)
         acc_d[...] = jnp.zeros_like(acc_d)
 
-    start = 0
-    for n_ref, dy_ref in zip(n_refs, dy_refs):
-        size = n_ref.shape[-2]
-        n_all[start:start + size, :] = n_ref[...].reshape(size, n_ref.shape[-1])
-        dy_all[start:start + size, :] = dy_ref[...].reshape(size, n_ref.shape[-1])
-        start += size
-    n_t[...] = n_all[...].T
-    dy_t[...] = dy_all[...].T
+    @pl.when(step == last // 2)
+    def _():
+        arrived(0, vo_all, left)
+        arrived(2, qk_all, right)
+        for copy in early() + swaps(far):
+            copy.start()
+
+    n_t[...] = n_ref[0].T
+    dy_t[...] = dy_ref[0].T
 
     @pl.loop(0, share // block)
     def _(i):
         cols = pl.ds(pl.multiple_of(i * block, block), block)
-        n, dy = n_all[...], dy_all[...]
+        n, dy = n_ref[0], dy_ref[0]
         hidden, d_gate, d_up = swiglu_both(dot_nn(n, wg_ref[:, cols]), dot_nn(n, wu_ref[:, cols]), dot_nt(dy, wd_ref[cols, :]))
         acc_g[:, cols] += dot_nn(n_t[...], d_gate)
         acc_u[:, cols] += dot_nn(n_t[...], d_up)
@@ -106,45 +127,54 @@
 
     @pl.when(step == last)
     def _():
-        for copy in swaps():
+        arrived(1, qk_all, left)
+        arrived(3, vo_all, right)
+        late_copies = late()
+        late_copies[0].start()
+        late_copies[1].start()
+        for copy in halves(share // block - 1):
+            copy.start()
+        arrived(6, vo_all, across)
+        late_copies[2].start()
+        arrived(7, qk_all, across)
+        late_copies[3].start()
+        for index, ref, slot in ((4, qk_all, partner), (5, vo_all, partner), (8, vo_all, other(left)), (9, qk_all, other(right)),
+                                 (10, qk_all, other(left)), (11, vo_all, other(right)), (12, vo_all, other(across)), (13, qk_all, other(across))):
+            arrived(index, ref, slot)
+        for copy in own() + early() + late_copies:
+            copy.wait_send()
+        for copy in swaps(near + far):
             copy.wait()
-        keep().wait()
-        for copy in halves(share // block - 1):
-            copy.start()
+        for copy in keep():
+            copy.wait()
         for i in range(share // block):
             for copy in halves(i):
                 copy.wait()
 
 
-def all_mlp(n_chunks, dy_chunks, w_gate, w_up, w_down, mix, block):
-    count, _, model = n_chunks[0][0].shape[-3:]
+def all_mlp(n, dy, w_gate, w_up, w_down, mix, qk, vo, block):
+    count, tile, model = n.shape
     share = w_gate.shape[1] // 2
-
-    def rows_of(part, which):
-        if part.ndim == 3:
-            return pl.BlockSpec((1,) + part.shape[1:], lambda i: (i, 0, 0))
-        return pl.BlockSpec((1, 1) + part.shape[2:], lambda i: (i, which, 0, 0))
-
-    chunks = n_chunks + dy_chunks
-    tile = sum(part.shape[-2] for part, _ in n_chunks)
+    tok = pl.BlockSpec((1, tile, model), lambda i: (i, 0, 0))
     one = pl.Buffered(1)
     core = lambda: lax.rem(lax.axis_index('sp'), 2)
     in_cols = pl.BlockSpec((model, share), lambda i: (0, core()), pipeline_mode=one)
     out_cols = pl.BlockSpec((model, share), lambda i: (0, 0), pipeline_mode=one)
     away = pl.BlockSpec(memory_space=pl.ANY)
     dma = pltpu.SemaphoreType.DMA
-    grads = [jax.ShapeDtypeStruct((model, share), BF16), jax.ShapeDtypeStruct((model, share), BF16), jax.ShapeDtypeStruct((share, model), BF16)]
+    shape = lambda *dims: jax.ShapeDtypeStruct(dims, BF16)
+    grads = [shape(model, share), shape(model, share), shape(share, model)]
     return pl.pallas_call(
-        functools.partial(all_mlp_kernel, chunks=len(n_chunks), block=block, count=count),
+        functools.partial(all_mlp_kernel, block=block, count=count),
         grid=(count,),
-        in_specs=[rows_of(*chunk) for chunk in chunks] + [in_cols, in_cols, pl.BlockSpec((share, model), lambda i: (core(), 0), pipeline_mode=one), away],
-        out_specs=[out_cols, out_cols, pl.BlockSpec((share, model), lambda i: (0, 0), pipeline_mode=one)] + [away] * 4,
-        out_shape=grads + grads + [jax.ShapeDtypeStruct(mix.shape, BF16)],
-        scratch_shapes=[pltpu.VMEM((tile, model), BF16)] * 2 + [pltpu.VMEM((model, tile), BF16)] * 2 + [pltpu.VMEM((model, share), F32)] * 3
-        + [dma((count - 1,)), dma((count - 1,)), dma((share // block, 3)), dma((share // block, 3)), dma],
+        in_specs=[tok, tok, in_cols, in_cols, pl.BlockSpec((share, model), lambda i: (core(), 0), pipeline_mode=one), away, away, away],
+        out_specs=[out_cols, out_cols, pl.BlockSpec((share, model), lambda i: (0, 0), pipeline_mode=one)] + [away] * 6,
+        out_shape=grads + grads + [shape(*mix.shape), shape(count, *qk.shape), shape(count, *vo.shape)],
+        scratch_shapes=[pltpu.VMEM((model, tile), BF16)] * 2 + [pltpu.VMEM((model, share), F32)] * 3
+        + [dma((count - 1,)), dma((count - 1,)), dma((share // block, 3)), dma((share // block, 3)), dma((14,)), dma((14,)), dma((3,))],
         compiler_params=pltpu.CompilerParams(vmem_limit_bytes=61 * 2 ** 20, collective_id=1, has_side_effects=True),
         cost_estimate=pl.CostEstimate(flops=12 * count * tile * model * share, bytes_accessed=4 * model * count * tile + 12 * model * share, transcendentals=0),
-    )(*[part for part, _ in chunks], w_gate, w_up, w_down, mix)
+    )(n, dy, w_gate, w_up, w_down, mix, qk, vo)
 
 
 def swap_pairs(rows):
@@ -239,7 +269,7 @@
 
 
 def front_kernel(n_ref, dy_ref, wg_ref, wu_ref, wd_ref, rope_ref, wq_ref, wk_ref, wv_ref, wo_ref, qn_ref, kn_ref,
-                 m_ref, dn_ref, gn_ref, gdy_ref, mix_ref, wn_ref, packed_ref,
+                 m_ref, dn_ref, gn_ref, gdy_ref, mix_ref, wn_ref, qk_ref, vo_ref,
                  n_all, dy_all, rope_all, m_acc, k_acc, v_acc, qkv_acc, o_acc, send_sem, recv_sem, rope_send, rope_recv, out_sem, *, count, blocks, heads, dim):
     step = pl.program_id(0)
     me = lax.axis_index('sp')
@@ -319,14 +349,15 @@
     @pl.when(step == 2)
     def _():
         pass_early(0)
-
-    @pl.when(step == 3)
-    def _():
         start_own(2)
 
+    @pl.when(step == blocks - 2)
+    def _():
+        pass_early(1)
+        start_own(3)
+
     @pl.when(step == blocks - 1)
     def _():
-        pass_early(1)
         pass_late(0)
 
     @pl.when(step < blocks)
@@ -360,9 +391,13 @@
     def _():
         seq = step - blocks
 
-        @pl.when(seq + 3 < batch)
+        @pl.when(seq + 2 < batch)
         def _():
-            start_own(seq + 3)
+            pass_early(seq + 2)
+
+        @pl.when(seq + 4 < batch)
+        def _():
+            start_own(seq + 4)
 
         @pl.when(seq + 1 < batch)
         def _():
@@ -375,17 +410,14 @@
         one_sequence(me, n_all[seq].reshape(full, model), dy_all[seq].reshape(full, model), rope_all[:, 0].reshape(full, dim), rope_all[:, 1].reshape(full, dim),
                      wq_ref, wk_ref, wv_ref, wo_ref, qn_ref, kn_ref, mix_ref, wn_ref, k_acc, v_acc, qkv_acc, o_acc, heads, dim, min(128, full))
 
-        @pl.when(seq + 2 < batch)
-        def _():
-            pass_early(seq + 2)
-
     @pl.when(step == pl.num_programs(0) - 1)
     def _():
-        qkv_size = qkv_acc.shape[0]
         size = o_acc.shape[0]
-        packed_ref[:, :qkv_size] = qkv_acc[...].T.astype(BF16)
+        qk_size = size + dim
+        qk_ref[...] = qkv_acc[:qk_size, :].T.astype(BF16)
+        vo_ref[:, :dim] = qkv_acc[qk_size:, :].T.astype(BF16)
         for i in range(model // size):
-            packed_ref[i * size:(i + 1) * size, qkv_size:] = o_acc[:, i * size:(i + 1) * size].astype(BF16)
+            vo_ref[i * size:(i + 1) * size, dim:] = o_acc[:, i * size:(i + 1) * size].astype(BF16)
 
         @pl.loop(0, batch)
         def _(seq):
@@ -418,9 +450,9 @@
                   mine(heads * dim), mine(dim), mine(dim), pl.BlockSpec((heads * dim, model), lambda i: (lax.axis_index('sp'), 0), pipeline_mode=one),
                   whole(q_norm.shape), whole(k_norm.shape)],
         out_specs=[whole((rows, model)), whole((rows, model)), away, away,
-                   pl.BlockSpec((count, 1, piece, width), lambda i: (0, jnp.maximum(i - blocks, 0), 0, 0)), whole((8, dim)), whole((model, width))],
+                   pl.BlockSpec((count, 1, piece, width), lambda i: (0, jnp.maximum(i - blocks, 0), 0, 0)), whole((8, dim)), whole((model, width // 2)), whole((model, width // 2))],
         out_shape=[shape((rows, model), BF16), shape((rows, model), F32), shape((batch, count, piece, model), BF16), shape((batch, count, piece, model), BF16),
-                   shape((count, batch, piece, width), BF16), shape((8, dim), F32), shape((model, width), BF16)],
+                   shape((count, batch, piece, width), BF16), shape((8, dim), F32), shape((model, width // 2), BF16), shape((model, width // 2), BF16)],
         scratch_shapes=[vmem((batch, count, piece, model), BF16), vmem((batch, count, piece, model), BF16), vmem((count,) + rope.shape, F32), vmem((rows, model), F32),
                         vmem((count * piece, dim), F32), vmem((count * piece, dim), F32), vmem(((heads + 2) * dim, model), F32), vmem((heads * dim, model), F32),
                         dma((batch, 14)), dma((batch, 14)), dma((count - 1,)), dma((count - 1,)), dma((batch, 2))],
@@ -449,8 +481,8 @@
     )(x, gain)
 
 
-def finish_kernel(core_ref, mix_ref, x_ref, dy_ref, m_ref, dn_ref, gain_ref, wq_ref, wk_ref, wv_ref, wo_ref, gg_ref, gu_ref, gd_ref, pg_ref, pu_ref, pd_ref,
-                  y_ref, dx_ref, gain_grad_ref, fg_ref, fu_ref, fd_ref, a_acc, d_acc, col_buf, row_buf, in_sem, out_sem, *, parts):
+def finish_kernel(core_ref, mix_ref, x_ref, dy_ref, m_ref, dn_ref, gain_ref, wq_ref, wk_ref, wv_ref, wo_ref, gg_ref, gu_ref, gd_ref, pg_ref, pu_ref, pd_ref, qk_ref, vo_ref,
+                  y_ref, dx_ref, gain_grad_ref, fg_ref, fu_ref, fd_ref, fq_ref, fk_ref, fv_ref, fo_ref, a_acc, d_acc, col_buf, row_buf, qk_buf, vo_buf, in_sem, out_sem, *, parts):
     step = pl.program_id(0)
     steps = pl.num_programs(0)
     o_size, k_size = parts
@@ -465,6 +497,7 @@
         rows = pl.ds(pl.multiple_of(at * row_rows, row_rows), row_rows)
         pairs = [(ref.at[cols], col_buf.at[slot, i]) for i, ref in enumerate((gg_ref, gu_ref, pg_ref, pu_ref))]
         pairs += [(ref.at[rows], row_buf.at[slot, i]) for i, ref in enumerate((gd_ref, pd_ref))]
+        pairs += [(qk_ref.at[at], qk_buf.at[slot]), (vo_ref.at[at], vo_buf.at[slot])]
         return [pltpu.make_async_copy(src, dst, in_sem.at[slot, i]) for i, (src, dst) in enumerate(pairs)]
 
     def places(at):
@@ -472,6 +505,10 @@
         cols = pl.ds(pl.multiple_of(at * col_rows, col_rows), col_rows)
         pairs = [(col_buf.at[slot, i], ref.at[cols, pl.ds(start, share)]) for i, (ref, start) in enumerate(((fg_ref, mine), (fu_ref, mine), (fg_ref, theirs), (fu_ref, theirs)))]
         pairs += [(row_buf.at[slot, i], fd_ref.at[pl.ds(pl.multiple_of(start + at * row_rows, row_rows), row_rows)]) for i, start in enumerate((mine, theirs))]
+        qk, vo = qk_buf.at[slot], vo_buf.at[slot]
+        at_o, at_k = pl.ds(pl.multiple_of(at * o_size, o_size), o_size), pl.ds(pl.multiple_of(at * k_size, k_size), k_size)
+        pairs += [(qk.at[:, pl.ds(0, o_size)], fq_ref.at[:, at_o]), (qk.at[:, pl.ds(o_size, k_size)], fk_ref.at[:, at_k]), (vo.at[:, pl.ds(0, k_size)], fv_ref.at[:, at_k])]
+        pairs += [(vo.at[pl.ds(i * o_size, o_size), pl.ds(k_size, o_size)], fo_ref.at[at_o, pl.ds(i * o_size, o_size)]) for i in range(qk.shape[0] // o_size)]
         return [pltpu.make_async_copy(src, dst, out_sem.at[slot, i]) for i, (src, dst) in enumerate(pairs)]
 
     @pl.when(step == 0)
@@ -529,7 +566,7 @@
             copy.wait()
 
 
-def finish(core, mix, x, dy, mlp_out, d_norm, gain, w_q, w_k, w_v, w_o, own_grads, partner_grads, o_size, k_size):
+def finish(core, mix, x, dy, mlp_out, d_norm, gain, w_q, w_k, w_v, w_o, own_grads, partner_grads, qk, vo, o_size, k_size):
     rows, model = x.shape
     pieces, _, width = mix.shape
     share = own_grads[0].shape[1]
@@ -545,54 +582,18 @@
             num_scalar_prefetch=1,
             grid=(pieces,),
             in_specs=[pl.BlockSpec((1, rows, width), lambda i, c: (i, 0, 0))] + [whole] * 4
-            + [row, cols(o_size), cols(k_size), cols(k_size), pl.BlockSpec((o_size, model), lambda i, c: (i, 0))] + [away] * 6,
-            out_specs=[whole, whole, pl.BlockSpec(gain_shape, lambda i, c: (0, 0))] + [away] * 3,
+            + [row, cols(o_size), cols(k_size), cols(k_size), pl.BlockSpec((o_size, model), lambda i, c: (i, 0))] + [away] * 8,
+            out_specs=[whole, whole, pl.BlockSpec(gain_shape, lambda i, c: (0, 0))] + [away] * 7,
             scratch_shapes=[pltpu.VMEM((rows, model), F32), pltpu.VMEM((rows, model), F32),
                             pltpu.VMEM((3, 4, model // pieces, share), BF16), pltpu.VMEM((3, 2, share // pieces, model), BF16),
-                            pltpu.SemaphoreType.DMA((3, 6)), pltpu.SemaphoreType.DMA((3, 6))],
+                            pltpu.VMEM((3,) + qk.shape[1:], BF16), pltpu.VMEM((3,) + vo.shape[1:], BF16),
+                            pltpu.SemaphoreType.DMA((3, 8)), pltpu.SemaphoreType.DMA((3, 9 + model // o_size))],
         ),
         out_shape=[bf16(rows, model), bf16(rows, model), jax.ShapeDtypeStruct(gain_shape, F32)]
-        + [bf16(model, 2 * share), bf16(model, 2 * share), bf16(2 * share, model)],
+        + [bf16(model, 2 * share), bf16(model, 2 * share), bf16(2 * share, model)] + [bf16(*weight.shape) for weight in (w_q, w_k, w_v, w_o)],
         compiler_params=pltpu.CompilerParams(vmem_limit_bytes=56 * 2 ** 20),
         cost_estimate=pl.CostEstimate(flops=2 * pieces * rows * width * model, bytes_accessed=14 * rows * model + 2 * pieces * width * (rows + model), transcendentals=0),
-    )(core, mix, x, dy, mlp_out, d_norm, gain, w_q, w_k, w_v, w_o, *own_grads, *partner_grads)
-
-
-def place_kernel(packed_ref, fq_ref, fk_ref, fv_ref, fo_ref, buf, in_sem, out_sem, *, o_size, k_size):
-    count, model, _ = packed_ref.shape
-    fetch = lambda at: pltpu.make_async_copy(packed_ref.at[at], buf.at[at], in_sem.at[at])
-
-    def places(at):
-        part = buf.at[at]
-        pairs = [(part.at[:, pl.ds(0, o_size)], fq_ref.at[:, pl.ds(at * o_size, o_size)]), (part.at[:, pl.ds(o_size, k_size)], fk_ref.at[:, pl.ds(at * k_size, k_size)]),
-                 (part.at[:, pl.ds(o_size + k_size, k_size)], fv_ref.at[:, pl.ds(at * k_size, k_size)])]
-        pairs += [(part.at[pl.ds(i * o_size, o_size), pl.ds(o_size + 2 * k_size, o_size)], fo_ref.at[pl.ds(at * o_size, o_size), pl.ds(i * o_size, o_size)])
-                  for i in range(model // o_size)]
-        return [pltpu.make_async_copy(src, dst, out_sem.at[at, i]) for i, (src, dst) in enumerate(pairs)]
-
-    for at in range(count):
-        fetch(at).start()
-    for at in range(count):
-        fetch(at).wait()
-        for copy in places(at):
-            copy.start()
-    for at in range(count):
-        for copy in places(at):
-            copy.wait()
-
-
-def place(packed, weights, o_size, k_size):
-    count, model, _ = packed.shape
-    away = pl.BlockSpec(memory_space=pl.ANY)
-    return pl.pallas_call(
-        functools.partial(place_kernel, o_size=o_size, k_size=k_size),
-        in_specs=[away],
-        out_specs=[away] * 4,
-        out_shape=[jax.ShapeDtypeStruct(weight.shape, BF16) for weight in weights],
-        scratch_shapes=[pltpu.VMEM(packed.shape, BF16), pltpu.SemaphoreType.DMA((count,)), pltpu.SemaphoreType.DMA((count, 3 + model // o_size))],
-        compiler_params=pltpu.CompilerParams(vmem_limit_bytes=40 * 2 ** 20),
-        cost_estimate=pl.CostEstimate(flops=2 ** 20, bytes_accessed=4 * packed.size, transcendentals=0),
-    )(packed)
+    )(core, mix, x, dy, mlp_out, d_norm, gain, w_q, w_k, w_v, w_o, *own_grads, *partner_grads, qk, vo)
 
 
 def share_kernel(gain_ref, norm_ref, gain_out, q_out, k_out, parts, send_sem, recv_sem, *, count, heads):
@@ -649,18 +650,14 @@
         sign = jnp.where(jnp.arange(dim) % 2 == 0, -1.0, 1.0).astype(F32)
         rope_own = jnp.stack([jnp.cos(angles), jnp.sin(angles) * sign[None, :]])
 
-        mlp_out, d_norm, n_all, dy_all, mix, norm_grads, packed = front(n_own, dy_own, w_gate, w_up, w_down, rope_own, w_q, w_k, w_v, w_o, q_norm, k_norm,
+        mlp_out, d_norm, n_all, dy_all, mix, norm_grads, qk, vo = front(n_own, dy_own, w_gate, w_up, w_down, rope_own, w_q, w_k, w_v, w_o, q_norm, k_norm,
                                                                         n_sp, piece, ffn // 6)
-        packed = lax.all_gather(packed, 'sp', axis=0, tiled=False)
-
         by_tile = lambda part: part.reshape(n_sp, -1, part.shape[-1])
-        *grads, mix = all_mlp([(by_tile(n_all), 0)], [(by_tile(dy_all), 0)], w_gate, w_up, w_down, by_tile(mix), ffn // 6)
-
-        y_out, grad_x, grad_gain, full_gate, full_up, full_down = finish((me % 2).reshape(1), mix, x_rows, dy_own, mlp_out, d_norm, gain_row, w_q, w_k, w_v, w_o,
-                                                                         grads[:3], grads[3:], heads * dim, dim)
+        *grads, mix, qk, vo = all_mlp(by_tile(n_all), by_tile(dy_all), w_gate, w_up, w_down, by_tile(mix), qk, vo, ffn // 6)
+
+        y_out, grad_x, grad_gain, full_gate, full_up, full_down, full_q, full_k, full_v, full_o = finish(
+            (me % 2).reshape(1), mix, x_rows, dy_own, mlp_out, d_norm, gain_row, w_q, w_k, w_v, w_o, grads[:3], grads[3:], qk, vo, heads * dim, dim)
         full_gain, full_qn, full_kn = share_small(grad_gain, norm_grads, q_norm, k_norm, n_sp)
-        packed, full_gain = lax.optimization_barrier((packed, full_gain))
-        full_q, full_k, full_v, full_o = place(packed, (w_q, w_k, w_v, w_o), heads * dim, dim)
         return (y_out.reshape(x_in.shape), grad_x.reshape(x_in.shape), full_q, full_k, full_v, full_o, full_gate, full_up, full_down,
                 full_gain.reshape(model), full_qn, full_kn)
 

time: 326 us -> 287 us (0.88)
  Pallas kernels: 303 us -> 281 us
  between operations: 14.2 us -> 0.73 us
    pallas_call x2 -> x1, Pallas kernels: 148 us -> 133 us  [all_mlp(): pl.pallas_call(functools.partial(all_mlp_kernel, block=block, count=count...]
    pallas_call x1, Pallas kernels: 120 us -> 105 us  [front(): pl.pallas_call(functools.partial(front_kernel, count=count, blocks=blocks...]
    pallas_call x1, Pallas kernels: 24.5 us -> 31.4 us  [finish(): pl.pallas_call(functools.partial(finish_kernel, parts=(o_size, k_size)),...]
  transfers between devices with their start and end apart: 1 -> 0, of which waited for: 0 -> 0; matrix products, arithmetic and copies ran while one was open for 0% -> 0% of each run, Pallas kernels for 53% -> 0%
where the time goes in v2:
time: 287 us
  Pallas kernels  281 us (98%)
  local copies, waits for them, and re-layouts  4.04 us (1%)
    pallas_call x1, Pallas kernels, all_mlp(): pl.pallas_call(functools.partial(all_mlp_kernel, block=block, count=count...  133 us
    pallas_call x1, Pallas kernels, front(): pl.pallas_call(functools.partial(front_kernel, count=count, blocks=blocks...  105 us
    pallas_call x1, Pallas kernels, finish(): pl.pallas_call(functools.partial(finish_kernel, parts=(o_size, k_size)),...  31.4 us
    pallas_call x1, Pallas kernels, share_small(): pl.pallas_call(functools.partial(share_kernel, count=count, heads=heads),...  7.66 us

profile of v2, /device:TPU:81, one launch (start us, length us, event | category | flops | bytes accessed | tf_op | source)
XLA Modules:
  0.0 286.9 jit_solution(4169578336460514106)
XLA Ops:
  0.7 0.7 convert_element_type.3
  1.3 0.2 multiply_cosine_fusion
  1.6 0.1 copy.26
  1.7 0.1 copy.25
  1.8 0.6 pad_maximum_fusion.rope_ref
  2.4 3.8 %shard_map.220.n_ref = bf16[512,1024]{1,0:T(8,128)(2,1)} custom-call(bf16[512,1024]{1,0:T(8,128)(2,1)} %bitcast.12, f32[1,1024]{1,0:T(1,128)} %bitcast.18), custom_call_target="tpu_custom_call" | custom-call | flops 4194304 | bytes 2097152 | tf_op jit(solution)/shard_map/pallas_call | solution.py:474
  6.2 105.2 %shard_map.221 = (bf16[512,1024]{1,0:T(8,128)(2,1)}, f32[512,1024]{1,0:T(8,128)}, bf16[8,8,64,1024]{3,2,1,0:T(8,128)(2,1)}, bf16[8,8,64,1024]{3,2,1,0:T(8,128)(2...) custom-call(bf16[512,1024]{1,0:T(8,128)(2,1)} %shard_map.220.n_ref, ...), custom_call_target="tpu_custom_call" | custom-call | flops 45097156608 | bytes 18874368 | tf_op jit(solution)/shard_map/pallas_call | solution.py:446
  111.4 132.5 %shard_map.222 = (bf16[1024,1536]{1,0:T(8,128)(2,1)}, bf16[1024,1536]{1,0:T(8,128)(2,1)}, bf16[1536,1024]{1,0:T(8,128)(2,1)}, bf16[1024,1536]{1,0:T(8,128)(2,1)}...) custom-call(bf16[8,512,1024]{2,1,0:T(8,128)(2,1)} %bitcast.23, ...), custom_call_target="tpu_custom_call" | custom-call | flops 77309411328 | bytes 35651584 | tf_op jit(solution)/shard_map/pallas_call | solution.py:167
  244.0 31.4 %shard_map.223 = (bf16[512,1024]{1,0:T(8,128)(2,1)}, bf16[512,1024]{1,0:T(8,128)(2,1)}, f32[8,128]{1,0:T(8,128)}, bf16[1024,3072]{1,0:T(8,128)(2,1)}, bf16[1024,...) custom-call(s32[1]{0:T(128)} %bitcast.core_ref, ...), custom_call_target="tpu_custom_call" | custom-call | flops 6442450944 | bytes 26214400 | tf_op jit(solution)/shard_map/pallas_call | solution.py:579
  275.4 7.7 %shard_map.224 = (f32[8,128]{1,0:T(8,128)}, f32[16,128]{1,0:T(8,128)}, f32[8,128]{1,0:T(8,128)}) custom-call(f32[8,128]{1,0:T(8,128)} %get-tuple-element.67.gain_ref, f32[8,128]{1,0:T(8,128)} %get-tuple-element.68.norm_ref), custom_call_target="tpu_custom_call" | custom-call | tf_op jit(solution)/shard_map/pallas_call | solution.py:622
  283.0 1.3 copy.30
  284.3 1.3 copy.31
  285.6 1.3 copy.32
  (5 shorter events, 0.1 us)

commit v3 on v2

--- a/solution.py
+++ b/solution.py
@@ -51,16 +51,15 @@
     right, left, across, partner = lax.rem(me + 2, count), lax.rem(me + count - 2, count), lax.rem(me + 4, count), me + 1 - 2 * lax.rem(me, 2)
     other = lambda device: device + 1 - 2 * lax.rem(device, 2)
 
+    tail = pl.ds(mix_ref.shape[1] - swap_ref.shape[1], swap_ref.shape[1])
+
     def swaps(shifts):
         copies = []
         for shift in shifts:
             device = lax.rem(me + shift, count)
-            copies.append(pltpu.make_async_remote_copy(src_ref=mix_ref.at[device], dst_ref=swap_ref.at[me], send_sem=swap_send.at[shift - 1], recv_sem=swap_recv.at[shift - 1],
+            copies.append(pltpu.make_async_remote_copy(src_ref=mix_ref.at[device, tail], dst_ref=swap_ref.at[me], send_sem=swap_send.at[shift - 1], recv_sem=swap_recv.at[shift - 1],
                                                        device_id={'sp': device}, device_id_type=MESH))
         return copies
-
-    near = [1, count - 1, 2, count - 2]
-    far = [shift for shift in range(3, count - 2)]
 
     def halves(i):
         cols = pl.ds(i * block, block)
@@ -82,24 +81,35 @@
                    send(3, vo_ref, vo_all, me, left), send(4, qk_ref, qk_all, me, partner), send(5, vo_ref, vo_all, me, partner)]
     early = lambda: [forward(6, vo_all, left, right), forward(7, qk_all, right, left), forward(8, vo_all, left, partner), forward(9, qk_all, right, partner)]
     late = lambda: [forward(10, qk_all, left, partner), forward(11, vo_all, right, partner), forward(12, vo_all, across, partner), forward(13, qk_all, across, partner)]
-    keep = lambda: [pltpu.make_async_copy(mix_ref.at[me], swap_ref.at[me], own_sem.at[0]), pltpu.make_async_copy(qk_ref, qk_all.at[me], own_sem.at[1]),
+    keep = lambda: [pltpu.make_async_copy(mix_ref.at[me, tail], swap_ref.at[me], own_sem.at[0]), pltpu.make_async_copy(qk_ref, qk_all.at[me], own_sem.at[1]),
                     pltpu.make_async_copy(vo_ref, vo_all.at[me], own_sem.at[2])]
 
     @pl.when(step == 0)
     def _():
         meet(count)
-        for copy in own() + swaps(near) + keep():
+        for copy in own() + swaps((1, count - 1, 2, count - 2)) + keep():
             copy.start()
         acc_g[...] = jnp.zeros_like(acc_g)
         acc_u[...] = jnp.zeros_like(acc_u)
         acc_d[...] = jnp.zeros_like(acc_d)
 
-    @pl.when(step == last // 2)
+    @pl.when(step == 2)
     def _():
         arrived(0, vo_all, left)
         arrived(2, qk_all, right)
-        for copy in early() + swaps(far):
-            copy.start()
+        for copy in early() + swaps(range(3, count - 2)):
+            copy.start()
+
+    def pass_late(parts):
+        copies = late()
+        for i in parts:
+            index, ref, slot = ((1, qk_all, left), (3, vo_all, right), (6, vo_all, across), (7, qk_all, across))[i]
+            arrived(index, ref, slot)
+            copies[i].start()
+
+    @pl.when(step == last - 1)
+    def _():
+        pass_late((0, 1))
 
     n_t[...] = n_ref[0].T
     dy_t[...] = dy_ref[0].T
@@ -127,23 +137,15 @@
 
     @pl.when(step == last)
     def _():
-        arrived(1, qk_all, left)
-        arrived(3, vo_all, right)
-        late_copies = late()
-        late_copies[0].start()
-        late_copies[1].start()
         for copy in halves(share // block - 1):
             copy.start()
-        arrived(6, vo_all, across)
-        late_copies[2].start()
-        arrived(7, qk_all, across)
-        late_copies[3].start()
+        pass_late((2, 3))
         for index, ref, slot in ((4, qk_all, partner), (5, vo_all, partner), (8, vo_all, other(left)), (9, qk_all, other(right)),
                                  (10, qk_all, other(left)), (11, vo_all, other(right)), (12, vo_all, other(across)), (13, qk_all, other(across))):
             arrived(index, ref, slot)
-        for copy in own() + early() + late_copies:
+        for copy in own() + early() + late():
             copy.wait_send()
-        for copy in swaps(near + far):
+        for copy in swaps(range(1, count)):
             copy.wait()
         for copy in keep():
             copy.wait()
@@ -152,7 +154,7 @@
                 copy.wait()
 
 
-def all_mlp(n, dy, w_gate, w_up, w_down, mix, qk, vo, block):
+def all_mlp(n, dy, w_gate, w_up, w_down, mix, lead, qk, vo, block):
     count, tile, model = n.shape
     share = w_gate.shape[1] // 2
     tok = pl.BlockSpec((1, tile, model), lambda i: (i, 0, 0))
@@ -169,7 +171,7 @@
         grid=(count,),
         in_specs=[tok, tok, in_cols, in_cols, pl.BlockSpec((share, model), lambda i: (core(), 0), pipeline_mode=one), away, away, away],
         out_specs=[out_cols, out_cols, pl.BlockSpec((share, model), lambda i: (0, 0), pipeline_mode=one)] + [away] * 6,
-        out_shape=grads + grads + [shape(*mix.shape), shape(count, *qk.shape), shape(count, *vo.shape)],
+        out_shape=grads + grads + [shape(count, mix.shape[1] - lead, *mix.shape[2:]), shape(count, *qk.shape), shape(count, *vo.shape)],
         scratch_shapes=[pltpu.VMEM((model, tile), BF16)] * 2 + [pltpu.VMEM((model, share), F32)] * 3
         + [dma((count - 1,)), dma((count - 1,)), dma((share // block, 3)), dma((share // block, 3)), dma((14,)), dma((14,)), dma((3,))],
         compiler_params=pltpu.CompilerParams(vmem_limit_bytes=61 * 2 ** 20, collective_id=1, has_side_effects=True),
@@ -269,8 +271,8 @@
 
 
 def front_kernel(n_ref, dy_ref, wg_ref, wu_ref, wd_ref, rope_ref, wq_ref, wk_ref, wv_ref, wo_ref, qn_ref, kn_ref,
-                 m_ref, dn_ref, gn_ref, gdy_ref, mix_ref, wn_ref, qk_ref, vo_ref,
-                 n_all, dy_all, rope_all, m_acc, k_acc, v_acc, qkv_acc, o_acc, send_sem, recv_sem, rope_send, rope_recv, out_sem, *, count, blocks, heads, dim):
+                 m_ref, dn_ref, gn_ref, gdy_ref, mix_ref, lead_ref, wn_ref, qk_ref, vo_ref,
+                 mix_buf, n_all, dy_all, rope_all, m_acc, k_acc, v_acc, qkv_acc, o_acc, send_sem, recv_sem, rope_send, rope_recv, out_sem, mix_sem, lead_send, lead_recv, lead_sem, *, count, blocks, heads, dim):
     step = pl.program_id(0)
     me = lax.axis_index('sp')
     right, left, across, partner = lax.rem(me + 2, count), lax.rem(me + count - 2, count), lax.rem(me + 4, count), me + 1 - 2 * lax.rem(me, 2)
@@ -329,6 +331,15 @@
 
     def to_memory(seq):
         return [pltpu.make_async_copy(n_all.at[seq], gn_ref.at[seq], out_sem.at[seq, 0]), pltpu.make_async_copy(dy_all.at[seq], gdy_ref.at[seq], out_sem.at[seq, 1])]
+
+    def mix_out(seq):
+        return pltpu.make_async_copy(mix_buf.at[lax.rem(seq, 2), :, 0], mix_ref.at[:, seq], mix_sem.at[lax.rem(seq, 2)])
+
+    def lead_swaps():
+        ahead = pl.ds(0, lead_ref.shape[1])
+        return [pltpu.make_async_copy(mix_ref.at[me, ahead], lead_ref.at[me], lead_sem)] + [
+            pltpu.make_async_remote_copy(src_ref=mix_ref.at[device, ahead], dst_ref=lead_ref.at[me], send_sem=lead_send.at[i], recv_sem=lead_recv.at[i],
+                                         device_id={'sp': device}, device_id_type=MESH) for i, device in enumerate(other_devices(count))]
 
     @pl.when(step == 0)
     def _():
@@ -403,12 +414,22 @@
         def _():
             pass_late(seq + 1)
 
+        @pl.when(seq > 1)
+        def _():
+            mix_out(seq - 2).wait()
+
+        @pl.when(seq == batch - 3)
+        def _():
+            for copy in lead_swaps():
+                copy.start()
+
         complete(seq)
         for copy in to_memory(seq):
             copy.start()
         full = count * piece
         one_sequence(me, n_all[seq].reshape(full, model), dy_all[seq].reshape(full, model), rope_all[:, 0].reshape(full, dim), rope_all[:, 1].reshape(full, dim),
-                     wq_ref, wk_ref, wv_ref, wo_ref, qn_ref, kn_ref, mix_ref, wn_ref, k_acc, v_acc, qkv_acc, o_acc, heads, dim, min(128, full))
+                     wq_ref, wk_ref, wv_ref, wo_ref, qn_ref, kn_ref, mix_buf.at[lax.rem(seq, 2)], wn_ref, k_acc, v_acc, qkv_acc, o_acc, heads, dim, min(128, full))
+        mix_out(seq).start()
 
     @pl.when(step == pl.num_programs(0) - 1)
     def _():
@@ -419,6 +440,11 @@
         for i in range(model // size):
             vo_ref[i * size:(i + 1) * size, dim:] = o_acc[:, i * size:(i + 1) * size].astype(BF16)
 
+        mix_out(batch - 2).wait()
+        mix_out(batch - 1).wait()
+        for copy in lead_swaps():
+            copy.wait()
+
         @pl.loop(0, batch)
         def _(seq):
             for copy in own(seq) + early(seq) + late(seq):
@@ -427,7 +453,7 @@
                 copy.wait()
 
 
-def front(n, dy, w_gate, w_up, w_down, rope, w_q, w_k, w_v, w_o, q_norm, k_norm, count, piece, block):
+def front(n, dy, w_gate, w_up, w_down, rope, w_q, w_k, w_v, w_o, q_norm, k_norm, count, piece, lead, block):
     rows, model = n.shape
     ffn = w_gate.shape[1]
     num_heads, dim = q_norm.shape
@@ -449,13 +475,12 @@
         in_specs=[whole((rows, model)), whole((rows, model)), cols, cols, pl.BlockSpec((block, model), lambda i: (jnp.minimum(i, blocks - 1), 0)), whole(rope.shape),
                   mine(heads * dim), mine(dim), mine(dim), pl.BlockSpec((heads * dim, model), lambda i: (lax.axis_index('sp'), 0), pipeline_mode=one),
                   whole(q_norm.shape), whole(k_norm.shape)],
-        out_specs=[whole((rows, model)), whole((rows, model)), away, away,
-                   pl.BlockSpec((count, 1, piece, width), lambda i: (0, jnp.maximum(i - blocks, 0), 0, 0)), whole((8, dim)), whole((model, width // 2)), whole((model, width // 2))],
+        out_specs=[whole((rows, model)), whole((rows, model)), away, away, away, away, whole((8, dim)), whole((model, width // 2)), whole((model, width // 2))],
         out_shape=[shape((rows, model), BF16), shape((rows, model), F32), shape((batch, count, piece, model), BF16), shape((batch, count, piece, model), BF16),
-                   shape((count, batch, piece, width), BF16), shape((8, dim), F32), shape((model, width // 2), BF16), shape((model, width // 2), BF16)],
-        scratch_shapes=[vmem((batch, count, piece, model), BF16), vmem((batch, count, piece, model), BF16), vmem((count,) + rope.shape, F32), vmem((rows, model), F32),
+                   shape((count, batch, piece, width), BF16), shape((count, lead, piece, width), BF16), shape((8, dim), F32), shape((model, width // 2), BF16), shape((model, width // 2), BF16)],
+        scratch_shapes=[vmem((2, count, 1, piece, width), BF16), vmem((batch, count, piece, model), BF16), vmem((batch, count, piece, model), BF16), vmem((count,) + rope.shape, F32), vmem((rows, model), F32),
                         vmem((count * piece, dim), F32), vmem((count * piece, dim), F32), vmem(((heads + 2) * dim, model), F32), vmem((heads * dim, model), F32),
-                        dma((batch, 14)), dma((batch, 14)), dma((count - 1,)), dma((count - 1,)), dma((batch, 2))],
+                        dma((batch, 14)), dma((batch, 14)), dma((count - 1,)), dma((count - 1,)), dma((batch, 2)), dma((2,)), dma((count - 1,)), dma((count - 1,)), dma],
         compiler_params=pltpu.CompilerParams(vmem_limit_bytes=62 * 2 ** 20, collective_id=0, has_side_effects=True),
         cost_estimate=pl.CostEstimate(flops=12 * rows * model * ffn + 8 * batch * count * piece * model * width, bytes_accessed=6 * model * ffn, transcendentals=0),
     )(n, dy, w_gate, w_up, w_down, rope, w_q, w_k, w_v, w_o, q_norm, k_norm)
@@ -481,8 +506,8 @@
     )(x, gain)
 
 
-def finish_kernel(core_ref, mix_ref, x_ref, dy_ref, m_ref, dn_ref, gain_ref, wq_ref, wk_ref, wv_ref, wo_ref, gg_ref, gu_ref, gd_ref, pg_ref, pu_ref, pd_ref, qk_ref, vo_ref,
-                  y_ref, dx_ref, gain_grad_ref, fg_ref, fu_ref, fd_ref, fq_ref, fk_ref, fv_ref, fo_ref, a_acc, d_acc, col_buf, row_buf, qk_buf, vo_buf, in_sem, out_sem, *, parts):
+def finish_kernel(core_ref, lead_ref, rest_ref, x_ref, dy_ref, m_ref, dn_ref, gain_ref, wq_ref, wk_ref, wv_ref, wo_ref, gg_ref, gu_ref, gd_ref, pg_ref, pu_ref, pd_ref, qk_ref, vo_ref,
+                  y_ref, dx_ref, gain_grad_ref, fg_ref, fu_ref, fd_ref, fq_ref, fk_ref, fv_ref, fo_ref, mix, a_acc, d_acc, col_buf, row_buf, qk_buf, vo_buf, in_sem, out_sem, *, parts):
     step = pl.program_id(0)
     steps = pl.num_programs(0)
     o_size, k_size = parts
@@ -526,7 +551,9 @@
         for copy in fetches(step + 1):
             copy.start()
 
-    mix = mix_ref[0]
+    lead = lead_ref.shape[1]
+    mix[:lead, :] = lead_ref[0]
+    mix[lead:, :] = rest_ref[0]
     a_new = dot_nn(mix[:, :o_size], wo_ref[...])
     d_new = dot_nt(mix[:, o_size:2 * o_size], wq_ref[...])
     d_new += dot_nt(mix[:, 2 * o_size:2 * o_size + k_size], wk_ref[...]) + dot_nt(mix[:, 2 * o_size + k_size:], wv_ref[...])
@@ -566,9 +593,9 @@
             copy.wait()
 
 
-def finish(core, mix, x, dy, mlp_out, d_norm, gain, w_q, w_k, w_v, w_o, own_grads, partner_grads, qk, vo, o_size, k_size):
+def finish(core, lead, rest, x, dy, mlp_out, d_norm, gain, w_q, w_k, w_v, w_o, own_grads, partner_grads, qk, vo, o_size, k_size):
     rows, model = x.shape
-    pieces, _, width = mix.shape
+    pieces, _, width = lead.shape
     share = own_grads[0].shape[1]
     whole = pl.BlockSpec((rows, model), lambda i, c: (0, 0))
     row = pl.BlockSpec((1, model), lambda i, c: (0, 0))
@@ -581,10 +608,10 @@
         grid_spec=pltpu.PrefetchScalarGridSpec(
             num_scalar_prefetch=1,
             grid=(pieces,),
-            in_specs=[pl.BlockSpec((1, rows, width), lambda i, c: (i, 0, 0))] + [whole] * 4
+            in_specs=[pl.BlockSpec((1, part.shape[1], width), lambda i, c: (i, 0, 0)) for part in (lead, rest)] + [whole] * 4
             + [row, cols(o_size), cols(k_size), cols(k_size), pl.BlockSpec((o_size, model), lambda i, c: (i, 0))] + [away] * 8,
             out_specs=[whole, whole, pl.BlockSpec(gain_shape, lambda i, c: (0, 0))] + [away] * 7,
-            scratch_shapes=[pltpu.VMEM((rows, model), F32), pltpu.VMEM((rows, model), F32),
+            scratch_shapes=[pltpu.VMEM((rows, width), BF16), pltpu.VMEM((rows, model), F32), pltpu.VMEM((rows, model), F32),
                             pltpu.VMEM((3, 4, model // pieces, share), BF16), pltpu.VMEM((3, 2, share // pieces, model), BF16),
                             pltpu.VMEM((3,) + qk.shape[1:], BF16), pltpu.VMEM((3,) + vo.shape[1:], BF16),
                             pltpu.SemaphoreType.DMA((3, 8)), pltpu.SemaphoreType.DMA((3, 9 + model // o_size))],
@@ -593,10 +620,10 @@
         + [bf16(model, 2 * share), bf16(model, 2 * share), bf16(2 * share, model)] + [bf16(*weight.shape) for weight in (w_q, w_k, w_v, w_o)],
         compiler_params=pltpu.CompilerParams(vmem_limit_bytes=56 * 2 ** 20),
         cost_estimate=pl.CostEstimate(flops=2 * pieces * rows * width * model, bytes_accessed=14 * rows * model + 2 * pieces * width * (rows + model), transcendentals=0),
-    )(core, mix, x, dy, mlp_out, d_norm, gain, w_q, w_k, w_v, w_o, *own_grads, *partner_grads, qk, vo)
-
-
-def share_kernel(gain_ref, norm_ref, gain_out, q_out, k_out, parts, send_sem, recv_sem, *, count, heads):
+    )(core, lead, rest, x, dy, mlp_out, d_norm, gain, w_q, w_k, w_v, w_o, *own_grads, *partner_grads, qk, vo)
+
+
+def share_kernel(gain_ref, norm_ref, parts, send_sem, recv_sem, *, count):
     me = lax.axis_index('sp')
     rows = gain_ref.shape[0]
     meet(count)
@@ -609,6 +636,12 @@
     parts[pl.ds(me, 1), rows:] = norm_ref[...][None]
     for copy in copies:
         copy.wait()
+
+
+def settle_kernel(parts, gain_out, q_out, k_out):
+    count = parts.shape[0]
+    rows = gain_out.shape[0]
+    heads = q_out.shape[0] // count
     gain_out[...] = jnp.sum(parts[:, :rows], axis=0)
     for device in range(count):
         q_out[device * heads:(device + 1) * heads, :] = parts[device, rows:rows + heads, :]
@@ -617,16 +650,21 @@
 
 def share_small(gain, norms, q_norm, k_norm, count):
     vmem = pl.BlockSpec(memory_space=pltpu.VMEM)
-    heads = q_norm.shape[0] // k_norm.shape[0]
     dma = pltpu.SemaphoreType.DMA((count - 1, 2))
+    parts = pl.pallas_call(
+        functools.partial(share_kernel, count=count),
+        in_specs=[vmem] * 2,
+        out_specs=vmem,
+        out_shape=jax.ShapeDtypeStruct((count, 2 * gain.shape[0], gain.shape[1]), F32),
+        scratch_shapes=[dma, dma],
+        compiler_params=pltpu.CompilerParams(collective_id=2, has_side_effects=True),
+    )(gain, norms)
     return pl.pallas_call(
-        functools.partial(share_kernel, count=count, heads=heads),
-        in_specs=[vmem] * 2,
+        settle_kernel,
+        in_specs=[vmem],
         out_specs=[vmem] * 3,
         out_shape=[jax.ShapeDtypeStruct(part.shape, F32) for part in (gain, q_norm, k_norm)],
-        scratch_shapes=[pltpu.VMEM((count, 2 * gain.shape[0], gain.shape[1]), F32), dma, dma],
-        compiler_params=pltpu.CompilerParams(collective_id=2, has_side_effects=True),
-    )(gain, norms)
+    )(parts)
 
 
 def solution(mesh):
@@ -641,6 +679,7 @@
         ffn = w_gate.shape[1]
         tokens = batch * piece
         me = lax.axis_index('sp')
+        ahead = batch // 4
         gain_row = norm_gain.reshape(1, model)
         x_rows, dy_own = x_in.reshape(tokens, model), grad_y.reshape(tokens, model)
         n_own = input_norm(x_rows, gain_row)
@@ -650,13 +689,13 @@
         sign = jnp.where(jnp.arange(dim) % 2 == 0, -1.0, 1.0).astype(F32)
         rope_own = jnp.stack([jnp.cos(angles), jnp.sin(angles) * sign[None, :]])
 
-        mlp_out, d_norm, n_all, dy_all, mix, norm_grads, qk, vo = front(n_own, dy_own, w_gate, w_up, w_down, rope_own, w_q, w_k, w_v, w_o, q_norm, k_norm,
-                                                                        n_sp, piece, ffn // 6)
+        mlp_out, d_norm, n_all, dy_all, mix, lead, norm_grads, qk, vo = front(n_own, dy_own, w_gate, w_up, w_down, rope_own, w_q, w_k, w_v, w_o, q_norm, k_norm,
+                                                                        n_sp, piece, ahead, ffn // 6)
         by_tile = lambda part: part.reshape(n_sp, -1, part.shape[-1])
-        *grads, mix, qk, vo = all_mlp(by_tile(n_all), by_tile(dy_all), w_gate, w_up, w_down, by_tile(mix), qk, vo, ffn // 6)
+        *grads, rest, qk, vo = all_mlp(by_tile(n_all), by_tile(dy_all), w_gate, w_up, w_down, mix, ahead, qk, vo, ffn // 6)
 
         y_out, grad_x, grad_gain, full_gate, full_up, full_down, full_q, full_k, full_v, full_o = finish(
-            (me % 2).reshape(1), mix, x_rows, dy_own, mlp_out, d_norm, gain_row, w_q, w_k, w_v, w_o, grads[:3], grads[3:], qk, vo, heads * dim, dim)
+            (me % 2).reshape(1), by_tile(lead), by_tile(rest), x_rows, dy_own, mlp_out, d_norm, gain_row, w_q, w_k, w_v, w_o, grads[:3], grads[3:], qk, vo, heads * dim, dim)
         full_gain, full_qn, full_kn = share_small(grad_gain, norm_grads, q_norm, k_norm, n_sp)
         return (y_out.reshape(x_in.shape), grad_x.reshape(x_in.shape), full_q, full_k, full_v, full_o, full_gate, full_up, full_down,
                 full_gain.reshape(model), full_qn, full_kn)

time: 287 us -> 277 us (0.965)
  Pallas kernels: 281 us -> 275 us
  local copies, waits for them, and re-layouts: 4.04 us -> 0.19 us
    pallas_call x1, Pallas kernels: 133 us -> 125 us  [all_mlp(): pl.pallas_call(functools.partial(all_mlp_kernel, block=block, count=count...]
    unnamed x3 -> x0, local copies, waits for them, and re-layouts: 3.85 us -> none
    pallas_call x1 -> x2, Pallas kernels: 7.66 us -> 8.17 us  [the longest x1 6.72 us: share_small(): pl.pallas_call(functools.partial(share_kernel, count=count), in_specs=[vm...]
where the time goes in v3:
time: 277 us
  Pallas kernels  275 us (99%)
    pallas_call x1, Pallas kernels, all_mlp(): pl.pallas_call(functools.partial(all_mlp_kernel, block=block, count=count...  125 us
    pallas_call x1, Pallas kernels, front(): pl.pallas_call(functools.partial(front_kernel, count=count, blocks=blocks...  106 us
    pallas_call x1, Pallas kernels, finish(): pl.pallas_call(functools.partial(finish_kernel, parts=(o_size, k_size)),...  31.5 us
    pallas_call x1, Pallas kernels, share_small(): pl.pallas_call(functools.partial(share_kernel, count=count), in_specs=[vm...  6.72 us

profile of v3, /device:TPU:81, one launch (start us, length us, event | category | flops | bytes accessed | tf_op | source)
XLA Modules:
  0.0 277.2 jit_solution(569533703169677824)
XLA Ops:
  0.7 0.7 convert_element_type.3
  1.3 0.2 multiply_cosine_fusion
  1.6 0.1 copy.26
  1.7 0.1 copy.25
  1.8 0.6 pad_maximum_fusion.rope_ref
  2.4 3.8 %shard_map.220.n_ref = bf16[512,1024]{1,0:T(8,128)(2,1)} custom-call(bf16[512,1024]{1,0:T(8,128)(2,1)} %bitcast.14, f32[1,1024]{1,0:T(1,128)} %bitcast.21), custom_call_target="tpu_custom_call" | custom-call | flops 4194304 | bytes 2097152 | tf_op jit(solution)/shard_map/pallas_call | solution.py:499
  6.2 105.9 %shard_map.221 = (bf16[512,1024]{1,0:T(8,128)(2,1)}, f32[512,1024]{1,0:T(8,128)}, bf16[8,8,64,1024]{3,2,1,0:T(8,128)(2,1)}, bf16[8,8,64,1024]{3,2,1,0:T(8,128)(2...) custom-call(bf16[512,1024]{1,0:T(8,128)(2,1)} %shard_map.220.n_ref, ...), custom_call_target="tpu_custom_call" | custom-call | flops 45097156608 | bytes 18874368 | tf_op jit(solution)/shard_map/pallas_call | solution.py:472
  112.1 125.4 %shard_map.222 = (bf16[1024,1536]{1,0:T(8,128)(2,1)}, bf16[1024,1536]{1,0:T(8,128)(2,1)}, bf16[1536,1024]{1,0:T(8,128)(2,1)}, bf16[1024,1536]{1,0:T(8,128)(2,1)}...) custom-call(bf16[8,512,1024]{2,1,0:T(8,128)(2,1)} %bitcast.26, ...), custom_call_target="tpu_custom_call" | custom-call | flops 77309411328 | bytes 35651584 | tf_op jit(solution)/shard_map/pallas_call | solution.py:169
  237.5 31.5 %shard_map.223 = (bf16[512,1024]{1,0:T(8,128)(2,1)}, bf16[512,1024]{1,0:T(8,128)(2,1)}, f32[8,128]{1,0:T(8,128)}, bf16[1024,3072]{1,0:T(8,128)(2,1)}, bf16[1024,...) custom-call(s32[1]{0:T(128)} %bitcast.core_ref, ...), custom_call_target="tpu_custom_call" | custom-call | flops 6442450944 | bytes 26214400 | tf_op jit(solution)/shard_map/pallas_call | solution.py:606
  269.0 6.7 %shard_map.224.parts = f32[8,16,128]{2,1,0:T(8,128)} custom-call(f32[8,128]{1,0:T(8,128)} %get-tuple-element.69.gain_ref, f32[8,128]{1,0:T(8,128)} %get-tuple-element.70.norm_ref), custom_call_target="tpu_custom_call" | custom-call | tf_op jit(solution)/shard_map/pallas_call | solution.py:654
  275.7 1.4 shard_map.225
  (5 shorter events, 0.1 us)
